TPU v7x, 32 devices: a 4x2x2 block of a 4x4x8 slice. The times are simulated.
32 devices in a mesh: dp: 4 (over y, z), tp: 8 (over x, core).
Axes of the slice: x: 4, y: 2, z: 2, core: 2. Of those that a mesh axis runs over, the one named last changes fastest.
The devices are a block of a 4x4x8 slice.
Arguments:
- y_one: float32 [32, 32, 2048], P('dp'), parts along dimension 0
- y_two: float32 [32, 32, 2048], P('dp'), parts along dimension 0
- dy_one: float32 [32, 32, 2048], P('dp'), parts along dimension 0
- dy_two: float32 [32, 32, 2048], P('dp'), parts along dimension 0
- seq_lens: int32 [32], P('dp'), parts along dimension 0
- w_query: bfloat16 [1, 2048, 16, 128], P(None, None, 'tp')
- w_key: bfloat16 [1, 2048, 8, 128], P(None, None, 'tp')
- w_value: bfloat16 [1, 2048, 8, 128], P(None, None, 'tp')
- w_out: bfloat16 [1, 16, 128, 2048], P(None, 'tp')
- w_up: bfloat16 [1, 2048, 8192], P(None, None, 'tp')
- w_down: bfloat16 [1, 8192, 2048], P(None, 'tp')
Outputs:
- output 1: float32 [32, 32, 2048], P('dp'), parts along dimension 0
- output 2: float32 [32, 32, 2048], P('dp'), parts along dimension 0
- output 3: float32 [32, 32, 2048], P('dp'), parts along dimension 0
- output 4: float32 [32, 32, 2048], P('dp'), parts along dimension 0
- output 5: float32 [4, 2048, 16, 128], P('dp', None, 'tp'), parts along dimension 0
- output 6: float32 [4, 2048, 8, 128], P('dp', None, 'tp'), parts along dimension 0
- output 7: float32 [4, 2048, 8, 128], P('dp', None, 'tp'), parts along dimension 0
- output 8: float32 [4, 16, 128, 2048], P('dp', 'tp'), parts along dimension 0
- output 9: float32 [4, 2048, 8192], P('dp', None, 'tp'), parts along dimension 0
- output 10: float32 [4, 8192, 2048], P('dp', 'tp'), parts along dimension 0
There are 4 independent parts. A program takes and returns all parts, laid end to end along the dimension named above; an argument that names none is the same for every part.
All inputs are finite; a program needn't handle non-finite values.
Results may differ from a plain program's by a relative error of at most 0.00909837.
Values are sent between devices in bfloat16 or wider.
A program may use at most 768 MiB of HBM per device.

v0:
```python
import jax
import jax.numpy as jnp
from jax import lax
from jax.sharding import PartitionSpec as P, NamedSharding

F32 = jnp.float32
BF16 = jnp.bfloat16
EPS = 1e-5
MASK_VALUE = -1e30


def rms_norm(x_val):
    inv_rms = lax.rsqrt(jnp.mean(x_val * x_val, axis=-1, keepdims=True) + EPS)
    return x_val * inv_rms, inv_rms


def rms_back(normed, inv_rms, grad_norm):
    return inv_rms * (grad_norm - normed * jnp.mean(grad_norm * normed, axis=-1, keepdims=True))


def visible_mask(seq_lens, seq_len):
    row_pos = lax.broadcasted_iota(jnp.int32, (seq_len, seq_len), 0)
    col_pos = lax.broadcasted_iota(jnp.int32, (seq_len, seq_len), 1)
    causal = (col_pos <= row_pos)[None, None, None]
    in_length = col_pos[None, None, None] < seq_lens[:, None, None, None, None]
    return causal & in_length


def block_back(carry, seq_lens, layer_w, all_reduce):
    y_one, y_two, dy_one, dy_two = carry
    w_query, w_key, w_value, w_out, w_up, w_down = layer_w
    n_batch, seq_len = y_one.shape[0], y_one.shape[1]
    n_heads, head_dim = w_query.shape[1], w_query.shape[2]
    kv_slots = w_key.shape[1]
    group_size = n_heads // kv_slots
    score_scale = head_dim ** -0.5

    norm_g, inv_g = rms_norm(y_one)
    norm_g_b = norm_g.astype(BF16)
    pre_act = jnp.einsum('bsd,df->bsf', norm_g_b, w_up, preferred_element_type=F32)
    act_val, gelu_back = jax.vjp(jax.nn.gelu, pre_act)
    act_b = act_val.astype(BF16)
    x_two = y_two - all_reduce(jnp.einsum('bsf,fd->bsd', act_b, w_down, preferred_element_type=F32))
    dy2_b = dy_two.astype(BF16)
    d_act = jnp.einsum('bsd,fd->bsf', dy2_b, w_down, preferred_element_type=F32)
    d_pre = gelu_back(d_act)[0].astype(BF16)
    dw_down = jnp.einsum('bsf,bsd->fd', act_b, dy2_b, preferred_element_type=F32)
    dw_up = jnp.einsum('bsd,bsf->df', norm_g_b, d_pre, preferred_element_type=F32)
    grad_norm_g = all_reduce(jnp.einsum('bsf,df->bsd', d_pre, w_up, preferred_element_type=F32))
    dy_one = dy_one + rms_back(norm_g, inv_g, grad_norm_g)

    norm_f, inv_f = rms_norm(x_two)
    norm_f_b = norm_f.astype(BF16)
    query_proj = jnp.einsum('bsd,dhe->bshe', norm_f_b, w_query, preferred_element_type=F32).astype(BF16)
    query_grp = query_proj.reshape(n_batch, seq_len, kv_slots, group_size, head_dim)
    key_proj = jnp.einsum('bsd,dge->bsge', norm_f_b, w_key, preferred_element_type=F32).astype(BF16)
    value_proj = jnp.einsum('bsd,dge->bsge', norm_f_b, w_value, preferred_element_type=F32).astype(BF16)
    scores = jnp.einsum('bigre,bjge->bgrij', query_grp, key_proj, preferred_element_type=F32) * score_scale
    scores = jnp.where(visible_mask(seq_lens, seq_len), scores, MASK_VALUE)
    attn_probs = jax.nn.softmax(scores, axis=-1)
    probs_b = attn_probs.astype(BF16)
    attn_out = jnp.einsum('bgrij,bjge->bigre', probs_b, value_proj, preferred_element_type=F32).astype(BF16)
    attn_out = attn_out.reshape(n_batch, seq_len, n_heads, head_dim)
    x_one = y_one - all_reduce(jnp.einsum('bihe,hed->bid', attn_out, w_out, preferred_element_type=F32))
    dy1_b = dy_one.astype(BF16)
    dw_out = jnp.einsum('bihe,bid->hed', attn_out, dy1_b, preferred_element_type=F32)
    d_attn = jnp.einsum('bid,hed->bihe', dy1_b, w_out, preferred_element_type=F32).astype(BF16)
    d_attn = d_attn.reshape(n_batch, seq_len, kv_slots, group_size, head_dim)
    d_value = jnp.einsum('bgrij,bigre->bjge', probs_b, d_attn, preferred_element_type=F32).astype(BF16)
    d_probs = jnp.einsum('bigre,bjge->bgrij', d_attn, value_proj, preferred_element_type=F32)
    d_scores = (attn_probs * (d_probs - jnp.sum(d_probs * attn_probs, axis=-1, keepdims=True)) * score_scale).astype(BF16)
    d_query = jnp.einsum('bgrij,bjge->bigre', d_scores, key_proj, preferred_element_type=F32).astype(BF16)
    d_query = d_query.reshape(n_batch, seq_len, n_heads, head_dim)
    d_key = jnp.einsum('bgrij,bigre->bjge', d_scores, query_grp, preferred_element_type=F32).astype(BF16)
    dw_query = jnp.einsum('bsd,bshe->dhe', norm_f_b, d_query, preferred_element_type=F32)
    dw_key = jnp.einsum('bsd,bsge->dge', norm_f_b, d_key, preferred_element_type=F32)
    dw_value = jnp.einsum('bsd,bsge->dge', norm_f_b, d_value, preferred_element_type=F32)
    grad_norm_f = all_reduce(jnp.einsum('bshe,dhe->bsd', d_query, w_query, preferred_element_type=F32)
                             + jnp.einsum('bsge,dge->bsd', d_key, w_key, preferred_element_type=F32)
                             + jnp.einsum('bsge,dge->bsd', d_value, w_value, preferred_element_type=F32))
    dx_two = dy_two + rms_back(norm_f, inv_f, grad_norm_f)
    return (x_one, x_two, dy_one, dx_two), (dw_query, dw_key, dw_value, dw_out, dw_up, dw_down)


def stack_grads(grads_by_layer):
    return tuple(jnp.stack([layer_grads[grad_pos] for layer_grads in grads_by_layer]) for grad_pos in range(6))


def tp_sum(partial_val):
    return lax.psum(partial_val, 'tp')


def solution(mesh):
    act_spec = P('dp', None, None)
    w_specs = (P(None, None, 'tp', None), P(None, None, 'tp', None), P(None, None, 'tp', None),
               P(None, 'tp', None, None), P(None, None, 'tp'), P(None, 'tp', None))
    g_specs = (P('dp', None, 'tp', None), P('dp', None, 'tp', None), P('dp', None, 'tp', None),
               P('dp', 'tp', None, None), P('dp', None, 'tp'), P('dp', 'tp', None))

    def local_fn(y_one, y_two, dy_one, dy_two, seq_lens, w_query, w_key, w_value, w_out, w_up, w_down):
        weights = (w_query, w_key, w_value, w_out, w_up, w_down)
        carry = (y_one, y_two, dy_one, dy_two)
        n_layers = w_query.shape[0]
        grads_by_layer = [None] * n_layers
        for layer_idx in reversed(range(n_layers)):
            layer_w = tuple(w_stack[layer_idx] for w_stack in weights)
            carry, grads_by_layer[layer_idx] = block_back(carry, seq_lens, layer_w, tp_sum)
        return carry + stack_grads(grads_by_layer)

    return jax.shard_map(local_fn, mesh=mesh,
                         in_specs=(act_spec,) * 4 + (P('dp'),) + w_specs,
                         out_specs=(act_spec,) * 4 + g_specs,
                         check_vma=False)
```

profile of v0, /device:TPU:81, one launch (start us, length us, event | category | flops | bytes accessed | tf_op | source)
XLA Modules:
  0.0 186.0 jit_solution(1685466652685977739)
XLA Ops:
  7.2 0.0 copy-start
  7.2 0.1 all-reduce.7.cloned.1.call-start
  7.3 2.0 %multiply_reduce_fusion.3 = f32[8,32]{1,0:T(8,128)S(1)} fusion(f32[8,32,2048]{2,1,0:T(8,128)} %param.11), kind=kLoop, calls=%fused_computation.21 | loop fusion | flops 1048320 | bytes 2098176 | tf_op jit(solution)/shard_map/reduce_sum | solution.py:13
  9.3 0.3 copy-done.2
  9.5 3.6 %fusion.6 = f32[8,32,1024]{2,1,0:T(8,128)S(1)} fusion(bf16[1,2048,1024]{2,1,0:T(8,128)(2,1)} %param.20, f32[8,32,2048]{2,1,0:T(8,128)S(1)} %copy-done.2, f32[8,32]{1,0:T(8,128)S(1)} %add_rsqrt_fusion.1), kind=kOutput, calls=%fused_computation.8 | convolution fusion | flops 1074790400 | bytes 7341056 | tf_op jit(solution)/shard_map/bsd,df->bsf/dot_general | solution.py:40
  13.1 0.0 copy-done.18
  13.2 0.0 copy-start.20
  13.2 0.0 copy-start.11
  13.2 2.7 %fusion.2 = f32[8,32,2048]{2,1,0:T(8,128)} fusion(bf16[1,1024,2048]{2,1,0:T(8,128)(2,1)S(1)} %copy-done.18, f32[8,32,1024]{2,1,0:T(8,128)S(1)} %fusion.6), kind=kOutput, calls=%fused_computation.4 | convolution fusion | flops 1076101120 | bytes 7340032 | tf_op jit(solution)/shard_map/bsf,fd->bsd/dot_general | solution.py:43
  15.9 1.8 fusion.24
  17.6 0.0 copy-start.22
  17.7 0.8 copy-done.22
  18.4 0.0 copy-done.19
  18.4 2.6 %fusion.4 = f32[8,32,2048]{2,1,0:T(8,128)} fusion(bf16[8,32,1024]{2,1,0:T(8,128)(2,1)S(1)} %fusion.24, bf16[1,2048,1024]{2,1,0:T(8,128)(2,1)S(1)} %copy-done.19), kind=kOutput, calls=%fused_computation.6 | convolution fusion | flops 1073741824 | bytes 6815744 | tf_op jit(solution)/shard_map/bsf,df->bsd/dot_general | solution.py:49
  21.1 0.1 all-reduce.7.cloned.1.call-update
  21.1 0.2 all-reduce.5.cloned.1.call-start
  21.4 0.3 copy-done.17
  21.7 0.1 fusion.50
  21.8 67.9 %all-reduce.7.cloned.1.call-done = (f32[8,32,2048]{2,1,0:T(8,128)}, f32[8,32,2048]{2,1,0:T(8,128)}) async-done(((f32[8,32,2048]{2,1,0:T(8,128)}, f32[8,32,2048]{2,1,0:T(8,128)}), (f32[8,32,2048]{2,1,0:T(8,128)}, f32[8,32,2048]{2,1,0:T(8,128)})) %all-reduce.7.cloned.1.call-update) | async-done | bytes 4194320 | tf_op jit(solution)/shard_map/psum | solution.py:90
  89.7 2.1 %multiply_reduce_fusion.1 = f32[8,32]{1,0:T(8,128)S(1)} fusion(f32[8,32,2048]{2,1,0:T(8,128)} %get-tuple-element.23, f32[8,32,2048]{2,1,0:T(8,128)S(1)} %copy-done.2, f32[8,32]{1,0:T(8,128)S(1)} %add_rsqrt_fusion.1), kind=kLoop, calls=%fused_computation.19 | loop fusion | flops 1572608 | bytes 4196352 | tf_op jit(solution)/shard_map/reduce_sum | solution.py:18
  91.8 0.1 copy-done.10
  91.9 0.6 copy-done.15
  92.6 2.9 %multiply_reduce_fusion.2 = (f32[8,32]{1,0:T(8,128)S(1)}, f32[8,32,2048]{2,1,0:T(8,128)S(1)}, f32[8,32,2048]{2,1,0:T(8,128)S(1)}) fusion(f32[8,32,2048]{2,1,0:T(8,128)S(1)} %copy-done.15, f32[8,32,2048]{2,1,0:T(8,128)} %get-tuple-element.22, f32[8,32,2048]{2,1,0:T(8,128)} %param.13, f32[8,32,2048]{2,1,0:T(8,128)S(1)} %copy-done.10, ...), kind=kLoop, calls=%fused_computation.20 | loop fusion | flops 4194048 | bytes 14683136 | tf_op jit(solution)/shard_map/reduce_sum | solution.py:13
  95.4 0.0 copy-start.3
  95.4 0.0 copy-start.5
  95.5 0.0 copy-start.13
  95.5 0.0 copy-start.14
  95.5 0.2 multiply_convert_fusion
  95.7 1.2 copy-done.13
  96.9 0.4 fusion.15
  97.3 0.0 copy-done.3
  97.3 0.1 copy-done.14
  97.5 0.4 fusion.14
  97.9 1.0 copy-done.16
  98.9 0.5 convolution_convert_fusion.3
  99.4 0.5 convolution_convert_fusion.2
  99.9 0.3 fusion.55
  100.2 0.1 fusion.46
  100.3 0.2 fusion.16
  100.5 0.3 fusion.10
  100.8 0.3 multiply_reduce_fusion.4
  101.1 0.1 fusion.47
  101.2 0.2 fusion.17
  101.4 0.2 fusion.11
  101.7 0.5 convolution_bitcast_fusion.3
  102.1 1.8 convolution_bitcast_fusion.4
  103.9 0.4 convolution_add_fusion.1
  104.3 1.8 convolution_add_fusion
  106.1 0.1 all-reduce.5.cloned.1.call-update
  106.2 1.2 copy-done.21
  107.3 6.5 %convolution_bitcast_fusion = f32[1,1024,2048]{2,1,0:T(8,128)} fusion(f32[8,32,2048]{2,1,0:T(8,128)} %param.14, f32[8,32,1024]{2,1,0:T(8,128)S(1)} %copy-done.21), kind=kOutput, calls=%fused_computation | convolution fusion | flops 1076625408 | bytes 11534336 | tf_op jit(solution)/shard_map/bsf,bsd->fd/dot_general | solution.py:47
  113.8 4.8 %convolution_bitcast_fusion.1 = f32[1,2048,1024]{2,1,0:T(8,128)} fusion(bf16[8,32,1024]{2,1,0:T(8,128)(2,1)S(1)} %copy-done.23, f32[8,32,2048]{2,1,0:T(8,128)S(1)} %copy-done.2, f32[8,32]{1,0:T(8,128)S(1)} %add_rsqrt_fusion.1), kind=kOutput, calls=%fused_computation.1 | convolution fusion | flops 1074790400 | bytes 11011072 | tf_op jit(solution)/shard_map/bsd,bsf->df/dot_general | solution.py:48
  118.6 0.0 copy-done.8
  118.6 0.5 convolution_bitcast_fusion.5
  119.1 8.8 %copy.27 = f32[1,2048,2,128]{3,2,1,0:T(2,128)} copy(f32[1,2048,2,128]{3,1,2,0:T(8,128)S(1)} %convolution_bitcast_fusion.5) | data formatting | bytes 4194304
  127.9 1.5 fusion.56
  129.3 1.5 fusion.57
  130.8 0.4 copy-done.6
  131.2 1.8 convolution_bitcast_fusion.2
  133.0 39.3 %all-reduce.5.cloned.1.call-done = (f32[8,32,2048]{2,1,0:T(8,128)}, f32[8,32,2048]{2,1,0:T(8,128)}) async-done(((f32[8,32,2048]{2,1,0:T(8,128)}, f32[8,32,2048]{2,1,0:T(8,128)}), (f32[8,32,2048]{2,1,0:T(8,128)}, f32[8,32,2048]{2,1,0:T(8,128)})) %all-reduce.5.cloned.1.call-update) | async-done | bytes 4194320 | tf_op jit(solution)/shard_map/psum | solution.py:90
  172.4 3.4 %sub.34 = f32[8,32,2048]{2,1,0:T(8,128)} subtract(f32[8,32,2048]{2,1,0:T(8,128)S(1)} %copy-done.2, f32[8,32,2048]{2,1,0:T(8,128)} %get-tuple-element.20) | non-fusion elementwise | flops 524288 | bytes 6291456 | tf_op jit(solution)/shard_map/sub | solution.py:64
  175.8 0.3 multiply_reduce_fusion
  176.1 1.2 copy-done.12
  177.4 1.8 multiply_add_fusion
  (30 shorter events, 0.1 us)
Async XLA Ops:
  7.2 92.2 %copy-start = (bf16[1,2,128,2048]{3,2,1,0:T(8,128)(2,1)S(1)}, bf16[1,2,128,2048]{3,2,1,0:T(8,128)(2,1)}, u32[]{:S(2)}) copy-start(bf16[1,2,128,2048]{3,2,1,0:T(8,128)(2,1)} %param.19) | copy-start | bytes 3145732
  7.2 2.3 %copy-start.2 = (f32[8,32,2048]{2,1,0:T(8,128)S(1)}, f32[8,32,2048]{2,1,0:T(8,128)}, u32[]{:S(2)}) copy-start(f32[8,32,2048]{2,1,0:T(8,128)} %param.11) | copy-start | bytes 6291460
  7.2 82.5 %all-reduce.7.cloned.1.call-start = ((), (), s32[]{:S(2)}) async-start(), calls=%async_computation.1 | async-start | bytes 8388608 | tf_op jit(solution)/shard_map/psum | solution.py:90
  9.5 3.6 %copy-start.18 = (bf16[1,1024,2048]{2,1,0:T(8,128)(2,1)S(1)}, bf16[1,1024,2048]{2,1,0:T(8,128)(2,1)}, u32[]{:S(2)}) copy-start(bf16[1,1024,2048]{2,1,0:T(8,128)(2,1)} %param.21) | copy-start | bytes 12582916
  13.2 2.7 %copy-start.20 = (f32[8,32,1024]{2,1,0:T(8,128)}, f32[8,32,1024]{2,1,0:T(8,128)S(1)}, u32[]{:S(2)}) copy-start(f32[8,32,1024]{2,1,0:T(8,128)S(1)} %fusion.6) | copy-start | bytes 3145732
  13.2 2.7 %copy-start.11 = (f32[8,32,2048]{2,1,0:T(8,128)S(1)}, f32[8,32,2048]{2,1,0:T(8,128)}, u32[]{:S(2)}) copy-start(f32[8,32,2048]{2,1,0:T(8,128)} %param.14) | copy-start | bytes 6291460
  15.9 2.6 %copy-start.19 = (bf16[1,2048,1024]{2,1,0:T(8,128)(2,1)S(1)}, bf16[1,2048,1024]{2,1,0:T(8,128)(2,1)}, u32[]{:S(2)}) copy-start(bf16[1,2048,1024]{2,1,0:T(8,128)(2,1)} %param.20) | copy-start | bytes 12582916
  17.6 0.8 copy-start.22
  21.1 0.7 copy-start.17
  21.1 151.2 %all-reduce.5.cloned.1.call-start = ((), (), s32[]{:S(2)}) async-start(), calls=%async_computation | async-start | bytes 8388608 | tf_op jit(solution)/shard_map/psum | solution.py:90
  89.7 2.2 %copy-start.10 = (f32[8,32,2048]{2,1,0:T(8,128)S(1)}, f32[8,32,2048]{2,1,0:T(8,128)}, u32[]{:S(2)}) copy-start(f32[8,32,2048]{2,1,0:T(8,128)} %get-tuple-element.23) | copy-start | bytes 6291460
  89.7 2.9 %copy-start.15 = (f32[8,32,2048]{2,1,0:T(8,128)S(1)}, f32[8,32,2048]{2,1,0:T(8,128)}, u32[]{:S(2)}) copy-start(f32[8,32,2048]{2,1,0:T(8,128)} %param.12) | copy-start | bytes 6291460
  95.4 1.9 %copy-start.3 = (f32[8,32,2048]{2,1,0:T(8,128)}, f32[8,32,2048]{2,1,0:T(8,128)S(1)}, u32[]{:S(2)}) copy-start(f32[8,32,2048]{2,1,0:T(8,128)S(1)} %get-tuple-element.25) | copy-start | bytes 6291460
  95.4 3.9 %copy-start.5 = (f32[8,32,2048]{2,1,0:T(8,128)}, f32[8,32,2048]{2,1,0:T(8,128)S(1)}, u32[]{:S(2)}) copy-start(f32[8,32,2048]{2,1,0:T(8,128)S(1)} %get-tuple-element.30) | copy-start | bytes 6291460
  95.5 1.4 copy-start.13
  95.5 2.0 %copy-start.14 = (bf16[1,2048,1,128]{3,1,2,0:T(8,128)(2,1)S(1)}, bf16[1,2048,1,128]{3,1,2,0:T(8,128)(2,1)}, u32[]{:S(2)}) copy-start(bf16[1,2048,1,128]{3,1,2,0:T(8,128)(2,1)} %param.18) | copy-start | bytes 1572868
  96.9 2.4 %copy-start.7 = (bf16[8,32,2048]{2,1,0:T(8,128)(2,1)}, bf16[8,32,2048]{2,1,0:T(8,128)(2,1)S(1)}, u32[]{:S(2)}) copy-start(bf16[8,32,2048]{2,1,0:T(8,128)(2,1)S(1)} %multiply_convert_fusion) | copy-start | bytes 3145732
  96.9 2.0 %copy-start.16 = (bf16[1,2048,2,128]{3,2,1,0:T(2,128)(2,1)S(1)}, bf16[1,2048,2,128]{3,2,1,0:T(2,128)(2,1)}, u32[]{:S(2)}) copy-start(bf16[1,2048,2,128]{3,2,1,0:T(2,128)(2,1)} %param.16) | copy-start | bytes 3145732
  106.1 1.2 copy-start.21
  107.3 6.5 %copy-start.23 = (bf16[8,32,1024]{2,1,0:T(8,128)(2,1)S(1)}, bf16[8,32,1024]{2,1,0:T(8,128)(2,1)}, u32[]{:S(2)}) copy-start(bf16[8,32,1024]{2,1,0:T(8,128)(2,1)} %copy-done.22) | copy-start | bytes 1572868
  113.8 4.8 %copy-start.8 = (bf16[8,32,2048]{2,1,0:T(8,128)(2,1)S(1)}, bf16[8,32,2048]{2,1,0:T(8,128)(2,1)}, u32[]{:S(2)}) copy-start(bf16[8,32,2048]{2,1,0:T(8,128)(2,1)} %copy-done.7) | copy-start | bytes 3145732
  129.3 1.9 %copy-start.6 = (f32[8,32,2048]{2,1,0:T(8,128)S(1)}, f32[8,32,2048]{2,1,0:T(8,128)}, u32[]{:S(2)}) copy-start(f32[8,32,2048]{2,1,0:T(8,128)} %copy-done.5) | copy-start | bytes 6291460
  172.3 3.4 %copy-start.4 = (f32[8,32,2048]{2,1,0:T(8,128)S(1)}, f32[8,32,2048]{2,1,0:T(8,128)}, u32[]{:S(2)}) copy-start(f32[8,32,2048]{2,1,0:T(8,128)} %copy-done.3) | copy-start | bytes 6291460
  172.4 3.4 %copy-start.9 = (f32[8,32,2048]{2,1,0:T(8,128)S(1)}, f32[8,32,2048]{2,1,0:T(8,128)}, u32[]{:S(2)}) copy-start(f32[8,32,2048]{2,1,0:T(8,128)} %get-tuple-element.21) | copy-start | bytes 6291460
  175.8 1.6 copy-start.12
  177.3 1.8 copy-start.1
Sparse Core Ops, SparseCore 0:
  21.2 68.4 all-reduce.6
  106.3 66.0 all-reduce.4
where the time goes:
time: 187 us; the launch traced here: 186 us
  waiting for transfers between devices  107 us (57%)
  matrix products  34.9 us (19%)
  local copies, waits for them, and re-layouts  16.2 us (9%)
  between operations  14.3 us (8%)
  other arithmetic  12.9 us (7%)
    psum x2, waiting for transfers between devices, tp_sum(): return lax.psum(partial_val, 'tp')  107 us
    unnamed x49, local copies, waits for them, and re-layouts  16.2 us
    dot_general x1, matrix products, block_back(): jnp.einsum('bsf,bsd->fd', act_b, dy2_b, preferred_element_type=F32)  6.48 us
    reduce_sum x2, other arithmetic, rms_norm(): inv_rms = lax.rsqrt(jnp.mean(x_val * x_val, axis=-1, keepdims=True) + EPS)  4.83 us
    dot_general x1, matrix products, block_back(): jnp.einsum('bsd,bsf->df', norm_g_b, d_pre, preferred_element_type=F32)  4.79 us
  transfers between devices with their start and end apart: 2, of which 2 were waited for; matrix products, arithmetic and copies ran while one was open for 14% of the time, Pallas kernels for 0%

commit v1 on v0

v1 whole, which is shorter than its diff:
```python
import functools
import jax
import jax.numpy as jnp
from jax import lax
from jax.experimental import pallas as pl
from jax.experimental.pallas import tpu as pltpu
from jax.sharding import PartitionSpec as P

F32 = jnp.float32
BF16 = jnp.bfloat16
EPS = 1e-5
MASK_VALUE = -1e30
GELU_C = 0.7978845608028654
GELU_A = 0.044715
MESH = pl.DeviceIdType.MESH
ANY = pl.BlockSpec(memory_space=pl.ANY)

N_CHUNKS = 4
N_SUMS = 4
N_MSGS = 12

LOAD_US = 2.5
MSG_US = ((1.5, 1.0),) + ((2.8, 1.9),) * 6 + ((5.6, 1.9),) * 2 + ((2.8, 1.9),) * 2 + ((1.5, 1.0),)
STEP_US = {'G1': 3.6, 'G2': 3.2, 'G3': 4.0, 'G4': 4.0, 'ATF': 8.0, 'ATO': 2.0, 'ATB': 9.6, 'ATG': 3.6}
SUM_US = {'F0': 0.03, 'F1': 0.2, 'F2R': 0.05, 'F2L': 0.05, 'F3': 0.25, 'F4R': 0.03, 'F4L': 0.03, 'F5': 0.03, 'F6': 0.03}
SENDS = {'F0': (0,), 'F1': (1, 2, 3, 4), 'F2R': (5,), 'F2L': (6,), 'F3': (7, 8), 'F4R': (9,), 'F4L': (10,), 'F5': (11,)}
RECVS = {'F1': (0,), 'F2R': (1,), 'F2L': (2,), 'F3': (3, 4, 5, 6), 'F4R': (7,), 'F4L': (8,), 'F5': (9, 10), 'F6': (11,)}
AFTER = {'F1': ('F0',), 'F2R': ('F1',), 'F2L': ('F1',), 'F3': ('F2R', 'F2L'), 'F4R': ('F3',), 'F4L': ('F3',),
         'F5': ('F4R', 'F4L'), 'F6': ('F5',)}
SOURCE = ('G2', 'G4', 'ATO', 'ATG')
NEEDS = {'G1': (), 'G2': ('G1',), 'G3': ('G1',), 'G4': ('G3',), 'ATF': (), 'ATO': ('ATF',), 'ATB': ('ATF',), 'ATG': ('ATB',)}
RANK = ('G1', 'G2', 'ATF', 'ATO', 'ATB', 'ATG', 'G3', 'G4')


def plan_order():
    todo = {}
    for c in range(N_CHUNKS):
        for name, pre in NEEDS.items():
            needs = [(p, c) for p in pre]
            if name in ('ATF', 'ATB'):
                needs.append(('F6', int(name == 'ATB'), c))
            todo[name, c] = (needs, STEP_US[name] / N_CHUNKS / 2, ())
        for a in range(N_SUMS):
            for name, cost in SUM_US.items():
                needs = [(p, a, c) for p in AFTER.get(name, ())] + [(i, a, c) for i in RECVS.get(name, ())]
                if name == 'F0':
                    needs.append((SOURCE[a], c))
                todo[name, a, c] = (needs, cost, SENDS.get(name, ()))

    def rank(key):
        if key[0] in STEP_US:
            pos = RANK.index(key[0])
            return (-1, key[1], pos) if pos < 2 else (1, pos, key[1])
        return (0,) + key[1:] + (key[0],)

    now, order, done, free = LOAD_US, [], {}, {}
    while todo:
        ready = {k: max([done[n] for n in v[0]], default=0.0) for k, v in todo.items() if all(n in done for n in v[0])}
        now = max(now, min(ready.values()))
        key = min((k for k, at in ready.items() if at <= now), key=rank)
        _, cost, sends = todo.pop(key)
        now += cost
        done[key] = now
        order.append(key)
        for i in sends:
            link = 0 if i in (0, 11) else 1 + i % 2
            wire, delay = MSG_US[i]
            start = max(now, free.get(link, 0.0))
            free[link] = start + wire / N_CHUNKS
            done[(i,) + key[1:]] = free[link] + delay
    return order


def mm(lhs, rhs):
    return jnp.dot(lhs, rhs, preferred_element_type=F32)


def mm_nt(lhs, rhs):
    return lax.dot_general(lhs, rhs, (((1,), (1,)), ((), ())), preferred_element_type=F32)


def mm_tn(lhs, rhs):
    return lax.dot_general(lhs, rhs, (((0,), (0,)), ((), ())), preferred_element_type=F32)


def inv_rms(x_val):
    return lax.rsqrt(jnp.mean(x_val * x_val, axis=-1, keepdims=True) + EPS)


def rms_back(x_val, grad_norm):
    inv = inv_rms(x_val)
    normed = x_val * inv
    return inv * (grad_norm - normed * jnp.mean(grad_norm * normed, axis=-1, keepdims=True))


def block_kernel(n_tp, head_dim, seq_len,
                 lens_ref, y1_hbm, y2_hbm, dy1_hbm, dy2_hbm, wq_hbm, wk_hbm, wv_hbm, wo_hbm, w1_hbm, w2_hbm,
                 x1_hbm, x2_hbm, dx1_hbm, dx2_hbm, ng_hbm, nf_hbm, act_hbm, dpre_hbm, attn_hbm, dqkv_hbm,
                 w1, w2, wqkv, wo, y1, dy2, y2_own, dy1_own, ng, nf, act, dact, dpre, qkv, prob, attn, dqkv,
                 part, d2d, ring1, ring2, full,
                 load_sem, out_sem, send_sem, recv_sem):
    tokens, width = y1.shape
    ff = w1.shape[1]
    qdim = attn.shape[1]
    n_heads = qdim // head_dim
    chunk = tokens // N_CHUNKS
    half = chunk // 2
    piece = half // (n_tp // 2)
    hw = width // 2
    n_chips = n_tp // 2

    me = lax.axis_index('tp')
    core = lax.rem(me, 2)
    chip = lax.div(me, 2)
    partner = me + 1 - 2 * core
    right = lax.rem(me + 2, n_tp)
    left = lax.rem(me + n_tp - 2, n_tp)
    chip_r = lax.rem(chip + 1, n_chips)
    chip_l = lax.rem(chip + n_chips - 1, n_chips)
    chip_o = lax.rem(chip + 2, n_chips)

    def half_rows(c, k):
        return pl.ds(pl.multiple_of(c * chunk + k * half, half), half)

    def piece_rows(c, x):
        return pl.ds(pl.multiple_of(c * chunk + core * half + x * piece, piece), piece)

    def own_rows(c):
        return pl.ds(c * piece, piece)

    lo, hi = pl.ds(0, hw), pl.ds(hw, hw)

    barrier = pltpu.get_barrier_semaphore()
    for dev in (partner, left, right):
        pl.semaphore_signal(barrier, inc=1, device_id={'tp': dev}, device_id_type=MESH)

    loads = {}

    def load(name, src, dst):
        loads[name] = pltpu.make_async_copy(src, dst, load_sem.at[len(loads)])
        loads[name].start()

    def arrived(*names):
        for name in names:
            if name in loads:
                loads.pop(name).wait()

    n_blk = ff // 256
    waits = []

    def load_all():
        c_rows = [pl.ds(c * chunk, chunk) for c in range(N_CHUNKS)]
        load_list = [(('y1', 0), y1_hbm.at[c_rows[0]], y1.at[c_rows[0]])]
        load_list += [(('w1', j), w1_hbm.at[:, pl.ds(j * 256, 256)], w1.at[:, pl.ds(j * 256, 256)]) for j in range(n_blk)]
        load_list += [(('y1', c), y1_hbm.at[c_rows[c]], y1.at[c_rows[c]]) for c in range(1, N_CHUNKS)]
        load_list += [(('w2',), w2_hbm, w2), (('dy2',), dy2_hbm, dy2)]
        for c in range(N_CHUNKS):
            load_list += [(('y2o', c), y2_hbm.at[piece_rows(c, chip)], y2_own.at[own_rows(c)]),
                          (('dy1o', c), dy1_hbm.at[piece_rows(c, chip)], dy1_own.at[own_rows(c)])]
        kv = head_dim
        load_list += [(('wqkv', 0), wq_hbm, wqkv.at[:, pl.ds(0, qdim)]),
                      (('wqkv', 1), wk_hbm, wqkv.at[:, pl.ds(qdim, kv)]),
                      (('wqkv', 2), wv_hbm, wqkv.at[:, pl.ds(qdim + kv, kv)]),
                      (('wo',), wo_hbm, wo)]
        for i, (name, src, dst) in enumerate(load_list):
            copy = pltpu.make_async_copy(src, dst, load_sem.at[i])
            copy.start()
            loads[name] = copy

    outs = []

    def store(src, dst):
        copy = pltpu.make_async_copy(src, dst, out_sem.at[len(outs)])
        copy.start()
        outs.append(copy)

    def msg(a, c, i):
        rows_own, rows_r, rows_l, rows_o = (piece_rows(c, x) for x in (chip, chip_r, chip_l, chip_o))
        u = a * N_CHUNKS + c
        slot = pl.ds(u * piece, piece)
        pa, oa = part.at[a], full.at[a]
        if i == 0:
            src, dst, dev = pa.at[half_rows(c, 1 - core)], d2d.at[pl.ds(u * half, half)], partner
        elif i == 1:
            src, dst, dev = pa.at[rows_o, lo], ring1.at[0, slot], right
        elif i == 2:
            src, dst, dev = pa.at[rows_o, hi], ring1.at[1, slot], left
        elif i == 3:
            src, dst, dev = pa.at[rows_r, hi], ring2.at[0, slot, hi], right
        elif i == 4:
            src, dst, dev = pa.at[rows_l, lo], ring2.at[1, slot, lo], left
        elif i == 5:
            src, dst, dev = pa.at[rows_r, lo], ring2.at[0, slot, lo], right
        elif i == 6:
            src, dst, dev = pa.at[rows_l, hi], ring2.at[1, slot, hi], left
        elif i == 7:
            src, dst, dev = oa.at[rows_own], oa.at[rows_own], right
        elif i == 8:
            src, dst, dev = oa.at[rows_own], oa.at[rows_own], left
        elif i == 9:
            src, dst, dev = oa.at[rows_l, lo], oa.at[rows_l, lo], right
        elif i == 10:
            src, dst, dev = oa.at[rows_r, hi], oa.at[rows_r, hi], left
        else:
            src, dst, dev = oa.at[half_rows(c, core)], oa.at[half_rows(c, core)], partner
        return pltpu.make_async_remote_copy(src, dst, send_sem.at[i, u], recv_sem.at[i, u],
                                            device_id={'tp': dev}, device_id_type=MESH)

    def send(a, c, *ids):
        for i in ids:
            msg(a, c, i).start()

    def recv(a, c, *ids):
        for i in ids:
            msg(a, c, i).wait_recv()

    state = {'met': False}

    def f0(a, c):
        if not state['met']:
            pl.semaphore_wait(barrier, 3)
            state['met'] = True
        send(a, c, 0)

    def f1(a, c):
        recv(a, c, 0)
        rows = half_rows(c, core)
        part[a, rows] = part[a, rows] + d2d[pl.ds((a * N_CHUNKS + c) * half, half)]
        send(a, c, 1, 2, 3, 4)

    def f2r(a, c):
        recv(a, c, 1)
        rows = piece_rows(c, chip_r)
        part[a, rows, lo] = part[a, rows, lo] + ring1[0, pl.ds((a * N_CHUNKS + c) * piece, piece)]
        send(a, c, 5)

    def f2l(a, c):
        recv(a, c, 2)
        rows = piece_rows(c, chip_l)
        part[a, rows, hi] = part[a, rows, hi] + ring1[1, pl.ds((a * N_CHUNKS + c) * piece, piece)]
        send(a, c, 6)

    def f3(a, c):
        recv(a, c, 3, 4, 5, 6)
        rows = piece_rows(c, chip)
        slot = pl.ds((a * N_CHUNKS + c) * piece, piece)
        total = part[a, rows] + ring2[0, slot] + ring2[1, slot]
        if a == 0:
            arrived(('y2o', c))
            out = y2_own[own_rows(c)] - total
        elif a == 1:
            arrived(('dy1o', c))
            out = dy1_own[own_rows(c)] + rms_back(y1[rows], total)
        elif a == 2:
            out = y1[rows] - total
        else:
            out = dy2[rows] + rms_back(full[0, rows], total)
        full[a, rows] = out
        send(a, c, 7, 8)

    def f4r(a, c):
        recv(a, c, 7)
        send(a, c, 9)

    def f4l(a, c):
        recv(a, c, 8)
        send(a, c, 10)

    def f5(a, c):
        recv(a, c, 9, 10)
        send(a, c, 11)

    def f6(a, c):
        recv(a, c, 11)
        rows = pl.ds(c * chunk, chunk)
        store(full.at[a, rows], (x2_hbm, dx1_hbm, x1_hbm, dx2_hbm)[a].at[rows])

    def g1(c):
        rows = pl.ds(c * chunk, chunk)
        arrived(('y1', c))
        y_val = y1[rows]
        ng[rows] = (y_val * inv_rms(y_val)).astype(BF16)
        store(ng.at[rows], ng_hbm.at[rows])

        def gelu_block(j):
            cols = pl.ds(pl.multiple_of(j * 256, 256), 256)
            pre = mm(ng[rows], w1[:, cols])
            inner = GELU_C * (pre + GELU_A * (pre * pre * pre))
            th = jnp.tanh(inner)
            act[rows, cols] = (0.5 * pre * (1.0 + th)).astype(BF16)
            dact[rows, cols] = 0.5 * (1.0 + th) + (0.5 * pre) * (1.0 - th * th) * (
                GELU_C * (1.0 + (3.0 * GELU_A) * (pre * pre)))

        if c == 0:
            for j in range(n_blk):
                arrived(('w1', j))
                gelu_block(j)
        else:
            pl.loop(0, n_blk)(gelu_block)
        store(act.at[rows], act_hbm.at[rows])

    def g2(c):
        rows = pl.ds(c * chunk, chunk)
        arrived(('w2',))

        @pl.loop(0, width // 512)
        def _(j):
            cols = pl.ds(pl.multiple_of(j * 512, 512), 512)
            part[0, rows, cols] = mm(act[rows], w2[:, cols])

    def g3(c):
        rows = pl.ds(c * chunk, chunk)
        arrived(('dy2',))

        @pl.loop(0, n_blk)
        def _(j):
            cols = pl.ds(pl.multiple_of(j * 256, 256), 256)
            d_act = mm_nt(dy2[rows].astype(BF16), w2[cols])
            dpre[rows, cols] = (dact[rows, cols] * d_act).astype(BF16)

        store(dpre.at[rows], dpre_hbm.at[rows])

    def g4(c):
        rows = pl.ds(c * chunk, chunk)

        @pl.loop(0, width // 256)
        def _(j):
            cols = pl.ds(pl.multiple_of(j * 256, 256), 256)
            part[1, rows, cols] = mm_nt(dpre[rows], w1[cols])

    def atf(c):
        rows = pl.ds(c * chunk, chunk)
        arrived(*(('wqkv', i) for i in range(3)))
        x_val = full[0, rows]
        nf[rows] = (x_val * inv_rms(x_val)).astype(BF16)
        store(nf.at[rows], nf_hbm.at[rows])
        qkv[rows] = mm(nf[rows], wqkv[...]).astype(BF16)
        key = qkv[rows, pl.ds(qdim, head_dim)]
        val = qkv[rows, pl.ds(qdim + head_dim, head_dim)]
        n_seqs = chunk // seq_len
        row_pos = lax.broadcasted_iota(jnp.int32, (chunk, chunk), 0)
        col_pos = lax.broadcasted_iota(jnp.int32, (chunk, chunk), 1)
        visible = jnp.zeros((chunk, chunk), jnp.bool_)
        for s in range(n_seqs):
            base = s * seq_len
            stop = base + lens_ref[c * n_seqs + s]
            visible = visible | ((row_pos >= base) & (row_pos < base + seq_len)
                                 & (col_pos >= base) & (col_pos < stop) & (col_pos <= row_pos))
        for h in range(n_heads):
            cols = pl.ds(h * head_dim, head_dim)
            scores = mm_nt(qkv[rows, cols], key) * (head_dim ** -0.5)
            scores = jnp.where(visible, scores, MASK_VALUE)
            exps = jnp.exp(scores - jnp.max(scores, axis=-1, keepdims=True))
            probs = exps / jnp.sum(exps, axis=-1, keepdims=True)
            prob[h, rows] = probs
            attn[rows, cols] = mm(probs.astype(BF16), val).astype(BF16)
        store(attn.at[rows], attn_hbm.at[rows])

    def ato(c):
        rows = pl.ds(c * chunk, chunk)
        arrived(('wo',))

        @pl.loop(0, width // 512)
        def _(j):
            cols = pl.ds(pl.multiple_of(j * 512, 512), 512)
            part[2, rows, cols] = mm(attn[rows], wo[:, cols])

    def atb(c):
        rows = pl.ds(c * chunk, chunk)
        d_attn = mm_nt(full[1, rows].astype(BF16), wo[...]).astype(BF16)
        key = qkv[rows, pl.ds(qdim, head_dim)]
        val = qkv[rows, pl.ds(qdim + head_dim, head_dim)]
        d_key = jnp.zeros((chunk, head_dim), F32)
        d_val = jnp.zeros((chunk, head_dim), F32)
        for h in range(n_heads):
            cols = pl.ds(h * head_dim, head_dim)
            d_head = d_attn[:, h * head_dim:(h + 1) * head_dim]
            probs = prob[h, rows]
            d_probs = mm_nt(d_head, val)
            d_scores = probs * (d_probs - jnp.sum(probs * d_probs, axis=-1, keepdims=True)) * (head_dim ** -0.5)
            d_scores = d_scores.astype(BF16)
            dqkv[rows, cols] = mm(d_scores, key).astype(BF16)
            d_key = d_key + mm_tn(d_scores, qkv[rows, cols])
            d_val = d_val + mm_tn(probs.astype(BF16), d_head)
        dqkv[rows, pl.ds(qdim, head_dim)] = d_key.astype(BF16)
        dqkv[rows, pl.ds(qdim + head_dim, head_dim)] = d_val.astype(BF16)
        store(dqkv.at[rows], dqkv_hbm.at[rows])

    def atg(c):
        rows = pl.ds(c * chunk, chunk)

        @pl.loop(0, width // 256)
        def _(j):
            cols = pl.ds(pl.multiple_of(j * 256, 256), 256)
            part[3, rows, cols] = mm_nt(dqkv[rows], wqkv[cols])

    steps = {'F0': f0, 'F1': f1, 'F2R': f2r, 'F2L': f2l, 'F3': f3, 'F4R': f4r, 'F4L': f4l, 'F5': f5, 'F6': f6,
             'G1': g1, 'G2': g2, 'G3': g3, 'G4': g4, 'ATF': atf, 'ATO': ato, 'ATB': atb, 'ATG': atg}
    load_all()
    for name, *where in plan_order():
        steps[name](*where)
    for copy in outs:
        copy.wait()
    for a in range(N_SUMS):
        for c in range(N_CHUNKS):
            for i in range(N_MSGS):
                msg(a, c, i).wait_send()


def block_call(n_tp, seq_lens, y_one, y_two, dy_one, dy_two, w_query, w_key, w_value, w_out, w_up, w_down):
    n_batch, seq_len, width = y_one.shape
    tokens = n_batch * seq_len
    n_heads, head_dim = w_query.shape[1], w_query.shape[2]
    ff = w_up.shape[1]
    qdim = n_heads * head_dim
    qkv_dim = qdim + 2 * head_dim
    chunk = tokens // N_CHUNKS
    units = N_SUMS * N_CHUNKS
    half = chunk // 2
    piece = half // (n_tp // 2)
    acts = tuple(v.reshape(tokens, width) for v in (y_one, y_two, dy_one, dy_two))
    weights = (w_query.reshape(width, qdim), w_key.reshape(width, head_dim), w_value.reshape(width, head_dim),
               w_out.reshape(qdim, width), w_up, w_down)
    sds = jax.ShapeDtypeStruct
    out_shape = [sds((tokens, width), F32)] * 4 + [
        sds((tokens, width), BF16), sds((tokens, width), BF16), sds((tokens, ff), BF16), sds((tokens, ff), BF16),
        sds((tokens, qdim), BF16), sds((tokens, qkv_dim), BF16)]
    vm = pltpu.VMEM
    scratch = [
        vm((width, ff), BF16), vm((ff, width), BF16), vm((width, qkv_dim), BF16), vm((qdim, width), BF16),
        vm((tokens, width), F32), vm((tokens, width), F32),
        vm((N_CHUNKS * piece, width), F32), vm((N_CHUNKS * piece, width), F32),
        vm((tokens, width), BF16), vm((tokens, width), BF16),
        vm((tokens, ff), BF16), vm((tokens, ff), F32), vm((tokens, ff), BF16),
        vm((tokens, qkv_dim), BF16), vm((n_heads, tokens, chunk), F32), vm((tokens, qdim), BF16),
        vm((tokens, qkv_dim), BF16),
        vm((N_SUMS, tokens, width), F32), vm((units * half, width), F32),
        vm((2, units * piece, width // 2), F32), vm((2, units * piece, width), F32),
        vm((N_SUMS, tokens, width), F32),
        pltpu.SemaphoreType.DMA((32,)), pltpu.SemaphoreType.DMA((48,)),
        pltpu.SemaphoreType.DMA((N_MSGS, units)), pltpu.SemaphoreType.DMA((N_MSGS, units)),
    ]
    return pl.pallas_call(
        functools.partial(block_kernel, n_tp, head_dim, seq_len),
        out_shape=out_shape,
        in_specs=[pl.BlockSpec(memory_space=pltpu.SMEM)] + [ANY] * 10,
        out_specs=[ANY] * len(out_shape),
        scratch_shapes=scratch,
        name='block_back',
        compiler_params=pltpu.CompilerParams(collective_id=0, has_side_effects=True,
                                             vmem_limit_bytes=60 * 1024 * 1024),
        cost_estimate=pl.CostEstimate(flops=10 ** 10, bytes_accessed=3 * 10 ** 7, transcendentals=10 ** 6),
    )(seq_lens, *acts, *weights)


def weight_grads(dy_two, dx1, ng, nf, act, dpre, attn, dqkv, n_heads, head_dim):
    qdim = n_heads * head_dim
    e_val, c_val = dy_two.astype(BF16), dx1.astype(BF16)
    dw_down = mm_tn(act, e_val)
    dw_up = mm_tn(ng, dpre)
    dw_out = mm_tn(attn, c_val)
    dw_query = mm_tn(nf, dqkv[:, :qdim])
    dw_key = mm_tn(nf, dqkv[:, qdim:qdim + head_dim])
    dw_value = mm_tn(nf, dqkv[:, qdim + head_dim:])
    return dw_query, dw_key, dw_value, dw_out, dw_up, dw_down


def solution(mesh):
    n_tp = mesh.shape['tp']
    act_spec = P('dp', None, None)
    w_specs = (P(None, None, 'tp', None), P(None, None, 'tp', None), P(None, None, 'tp', None),
               P(None, 'tp', None, None), P(None, None, 'tp'), P(None, 'tp', None))
    g_specs = (P('dp', None, 'tp', None), P('dp', None, 'tp', None), P('dp', None, 'tp', None),
               P('dp', 'tp', None, None), P('dp', None, 'tp'), P('dp', 'tp', None))

    def local_fn(y_one, y_two, dy_one, dy_two, seq_lens, w_query, w_key, w_value, w_out, w_up, w_down):
        n_heads, head_dim = w_query.shape[2], w_query.shape[3]
        tokens, width = y_one.shape[0] * y_one.shape[1], y_one.shape[2]
        ws = tuple(w[0] for w in (w_query, w_key, w_value, w_out, w_up, w_down))
        x1, x2, dx1, dx2, ng, nf, act, dpre, attn, dqkv = block_call(
            n_tp, seq_lens, y_one, y_two, dy_one, dy_two, *ws)
        dw = weight_grads(dy_two.reshape(tokens, width), dx1, ng, nf, act, dpre, attn, dqkv, n_heads, head_dim)
        dw = tuple(g.reshape((1,) + w.shape) for g, w in zip(dw, ws))
        return tuple(v.reshape(y_one.shape) for v in (x1, x2, dx1, dx2)) + dw

    return jax.shard_map(local_fn, mesh=mesh,
                         in_specs=(act_spec,) * 4 + (P('dp'),) + w_specs,
                         out_specs=(act_spec,) * 4 + g_specs,
                         check_vma=False)
```

time: 187 us -> 144 us (0.77)
  Pallas kernels: 0 us -> 112 us
  waiting for transfers between devices: 107 us -> 0 us
  matrix products: 34.9 us -> 17.2 us
  between operations: 14.3 us -> 0.7 us
  other arithmetic: 12.9 us -> 0 us
  local copies, waits for them, and re-layouts: 16.2 us -> 14 us
    pallas_call x0 -> x1, Pallas kernels: none -> 112 us  [block_call(): pl.pallas_call(functools.partial(block_kernel, n_tp, head_dim, seq_len),...]
    psum x2 -> x0, waiting for transfers between devices: 107 us -> none  [tp_sum(): return lax.psum(partial_val, 'tp')]
    dot_general x24 -> x6, matrix products: 34.9 us -> 17.2 us  [mm_tn(): lax.dot_general(lhs, rhs, (((0,), (0,)), ((), ())), preferred_element_typ...]
    reduce_sum x5 -> x0, other arithmetic: 7.34 us -> none  [the longest x2 4.83 us: rms_norm(): inv_rms = lax.rsqrt(jnp.mean(x_val * x_val, axis=-1, keepdims=True) + EPS)]
    sub x1 -> x0, other arithmetic: 3.4 us -> none  [block_back(): y_one - all_reduce(jnp.einsum('bihe,hed->bid', attn_out, w_out, preferred...]
    unnamed x49 -> x28, local copies, waits for them, and re-layouts: 16.2 us -> 14 us
  transfers between devices with their start and end apart: 2 -> 0, of which waited for: 2 -> 0; matrix products, arithmetic and copies ran while one was open for 14% -> 0% of each run, Pallas kernels for 0% -> 0%
where the time goes in v1:
time: 144 us
  Pallas kernels  112 us (78%)
  matrix products  17.2 us (12%)
  local copies, waits for them, and re-layouts  14 us (10%)
    pallas_call x1, Pallas kernels, block_call(): pl.pallas_call(functools.partial(block_kernel, n_tp, head_dim, seq_len),...  112 us
    dot_general x6, matrix products, mm_tn(): lax.dot_general(lhs, rhs, (((0,), (0,)), ((), ())), preferred_element_typ...  17.2 us
    unnamed x28, local copies, waits for them, and re-layouts  14 us

profile of v1, /device:TPU:81, one launch (start us, length us, event | category | flops | bytes accessed | tf_op | source)
XLA Modules:
  0.0 143.8 jit_solution(16587235785297809667)
XLA Ops:
  0.6 2.3 %copy.26 = bf16[256,8,2,128]{3,1,2,0:T(8,128)(2,1)} copy(bf16[256,8,2,128]{3,2,1,0:T(2,128)(2,1)} %bitcast.45) | data formatting | bytes 2097152
  3.0 111.9 %block_back.1 = (f32[256,2048]{1,0:T(8,128)}, f32[256,2048]{1,0:T(8,128)}, f32[256,2048]{1,0:T(8,128)}, f32[256,2048]{1,0:T(8,128)}, bf16[256,2048]{1,0:T(8,128)...) custom-call(s32[8]{0:T(128)} %lens_ref.1, ...), custom_call_target="tpu_custom_call" | custom-call | flops 10000000000 | bytes 30000000 | tf_op jit(solution)/shard_map/block_back/pallas_call | solution.py:443
  114.9 0.0 copy-start
  114.9 0.0 copy-start.9
  114.9 2.8 %fusion.5 = f32[2048,128]{1,0:T(8,128)} fusion(bf16[256,2048]{1,0:T(8,128)(2,1)} %get-tuple-element.24, bf16[256,512]{1,0:T(8,128)(2,1)} %get-tuple-element.25), kind=kOutput, calls=%fused_computation.8 | convolution fusion | flops 134217728 | bytes 2162688 | tf_op jit(solution)/shard_map/dot_general | solution.py:83
  117.7 0.0 copy-done
  117.7 0.0 copy-done.9
  117.7 1.5 %fusion.7 = f32[2048,128]{1,0:T(8,128)} fusion(bf16[256,2048]{1,0:T(8,128)(2,1)S(1)} %copy-done, bf16[256,512]{1,0:T(8,128)(2,1)S(1)} %copy-done.9), kind=kOutput, calls=%fused_computation.10 | convolution fusion | flops 134217728 | bytes 2162688 | tf_op jit(solution)/shard_map/dot_general | solution.py:83
  119.1 1.8 %fusion.3 = f32[2048,256]{0,1:T(8,128)} fusion(bf16[256,2048]{1,0:T(8,128)(2,1)S(1)} %copy-done, bf16[256,512]{1,0:T(8,128)(2,1)S(1)} %copy-done.9), kind=kOutput, calls=%fused_computation.6 | convolution fusion | flops 268435456 | bytes 3276800 | tf_op jit(solution)/shard_map/dot_general | solution.py:83
  121.0 0.0 copy-start.1
  121.0 0.0 copy-start.10
  121.0 4.3 %copy.21 = f32[1,2048,2,128]{3,2,1,0:T(2,128)} copy(f32[1,2048,2,128]{1,3,2,0:T(8,128)} %bitcast.38) | data formatting | bytes 4194304
  125.2 0.0 copy-done.1
  125.2 0.0 copy-done.10
  125.2 0.0 copy-start.6
  125.2 0.0 copy-start.8
  125.2 1.8 %fusion.1 = f32[256,2048]{1,0:T(8,128)} fusion(bf16[256,256]{1,0:T(8,128)(2,1)S(1)} %copy-done.10, f32[256,2048]{1,0:T(8,128)S(1)} %copy-done.1), kind=kOutput, calls=%fused_computation.4 | convolution fusion | flops 268959744 | bytes 4325376 | tf_op jit(solution)/shard_map/dot_general | solution.py:83
  127.0 0.0 copy-done.6
  127.0 0.0 copy-done.8
  127.0 0.0 copy-start.5
  127.0 0.0 copy-start.7
  127.0 4.7 %convolution_bitcast_fusion.1 = f32[1,2048,1024]{2,1,0:T(8,128)} fusion(bf16[256,2048]{1,0:T(8,128)(2,1)S(1)} %copy-done.6, bf16[256,1024]{1,0:T(8,128)(2,1)S(1)} %copy-done.8), kind=kOutput, calls=%fused_computation.1 | convolution fusion | flops 1073741824 | bytes 9961472 | tf_op jit(solution)/shard_map/dot_general | solution.py:83
  131.7 0.0 copy-done.5
  131.7 0.0 copy-done.7
  131.7 0.0 copy-start.4
  131.7 4.7 %convolution_bitcast_fusion = f32[1,1024,2048]{2,1,0:T(8,128)} fusion(bf16[256,1024]{1,0:T(8,128)(2,1)S(1)} %copy-done.7, f32[256,2048]{1,0:T(8,128)S(1)} %bitcast.44), kind=kOutput, calls=%fused_computation | convolution fusion | flops 1074266112 | bytes 11010048 | tf_op jit(solution)/shard_map/dot_general | solution.py:83
  136.4 0.0 copy-done.4
  136.4 0.0 copy-start.3
  136.4 1.3 copy.31
  137.7 1.0 copy-done.3
  138.8 1.3 copy.32
  140.1 0.0 copy-start.2
  140.1 1.3 copy.33
  141.4 1.0 copy-done.2
  142.4 1.3 copy.34
Async XLA Ops:
  114.9 2.8 %copy-start = (bf16[256,2048]{1,0:T(8,128)(2,1)S(1)}, bf16[256,2048]{1,0:T(8,128)(2,1)}, u32[]{:S(2)}) copy-start(bf16[256,2048]{1,0:T(8,128)(2,1)} %get-tuple-element.24) | copy-start | bytes 3145732
  114.9 2.8 %copy-start.9 = (bf16[256,512]{1,0:T(8,128)(2,1)S(1)}, bf16[256,512]{1,0:T(8,128)(2,1)}, u32[]{:S(2)}) copy-start(bf16[256,512]{1,0:T(8,128)(2,1)} %get-tuple-element.25) | copy-start | bytes 786436
  121.0 4.3 %copy-start.1 = (f32[256,2048]{1,0:T(8,128)S(1)}, f32[256,2048]{1,0:T(8,128)}, u32[]{:S(2)}) copy-start(f32[256,2048]{1,0:T(8,128)} %get-tuple-element.22) | copy-start | bytes 6291460
  121.0 4.3 %copy-start.10 = (bf16[256,256]{1,0:T(8,128)(2,1)S(1)}, bf16[256,256]{1,0:T(8,128)(2,1)}, u32[]{:S(2)}) copy-start(bf16[256,256]{1,0:T(8,128)(2,1)} %get-tuple-element.26) | copy-start | bytes 393220
  125.2 1.8 %copy-start.6 = (bf16[256,2048]{1,0:T(8,128)(2,1)S(1)}, bf16[256,2048]{1,0:T(8,128)(2,1)}, u32[]{:S(2)}) copy-start(bf16[256,2048]{1,0:T(8,128)(2,1)} %get-tuple-element.27) | copy-start | bytes 3145732
  125.2 1.8 %copy-start.8 = (bf16[256,1024]{1,0:T(8,128)(2,1)S(1)}, bf16[256,1024]{1,0:T(8,128)(2,1)}, u32[]{:S(2)}) copy-start(bf16[256,1024]{1,0:T(8,128)(2,1)} %get-tuple-element.28) | copy-start | bytes 1572868
  127.0 4.7 %copy-start.5 = (f32[8,32,2048]{2,1,0:T(8,128)S(1)}, f32[8,32,2048]{2,1,0:T(8,128)}, u32[]{:S(2)}) copy-start(f32[8,32,2048]{2,1,0:T(8,128)} %param.14) | copy-start | bytes 6291460
  127.0 4.7 %copy-start.7 = (bf16[256,1024]{1,0:T(8,128)(2,1)S(1)}, bf16[256,1024]{1,0:T(8,128)(2,1)}, u32[]{:S(2)}) copy-start(bf16[256,1024]{1,0:T(8,128)(2,1)} %get-tuple-element.29) | copy-start | bytes 1572868
  131.7 4.7 %copy-start.4 = (f32[256,2048]{1,0:T(8,128)S(1)}, f32[256,2048]{1,0:T(8,128)}, u32[]{:S(2)}) copy-start(f32[256,2048]{1,0:T(8,128)} %get-tuple-element.20) | copy-start | bytes 6291460
  136.4 2.3 %copy-start.3 = (f32[256,2048]{1,0:T(8,128)S(1)}, f32[256,2048]{1,0:T(8,128)}, u32[]{:S(2)}) copy-start(f32[256,2048]{1,0:T(8,128)} %get-tuple-element.21) | copy-start | bytes 6291460
  140.1 2.3 %copy-start.2 = (f32[256,2048]{1,0:T(8,128)S(1)}, f32[256,2048]{1,0:T(8,128)}, u32[]{:S(2)}) copy-start(f32[256,2048]{1,0:T(8,128)} %get-tuple-element.23) | copy-start | bytes 6291460

commit v2 on v1

--- a/solution.py
+++ b/solution.py
@@ -16,41 +16,53 @@
 ANY = pl.BlockSpec(memory_space=pl.ANY)
 
 N_CHUNKS = 4
+N_GROUPS = 2
+N_PARTS = 2
 N_SUMS = 4
 N_MSGS = 12
 
-LOAD_US = 2.5
-MSG_US = ((1.5, 1.0),) + ((2.8, 1.9),) * 6 + ((5.6, 1.9),) * 2 + ((2.8, 1.9),) * 2 + ((1.5, 1.0),)
-STEP_US = {'G1': 3.6, 'G2': 3.2, 'G3': 4.0, 'G4': 4.0, 'ATF': 8.0, 'ATO': 2.0, 'ATB': 9.6, 'ATG': 3.6}
+LOAD_US = 3.5
+STEP_US = {'G1': 1.0, 'G2': 0.9, 'G3': 0.9, 'G4': 0.6, 'PREP': 1.0, 'ATF': 1.6, 'ATO': 0.6, 'ATB': 2.0, 'ATG': 1.2}
 SUM_US = {'F0': 0.03, 'F1': 0.2, 'F2R': 0.05, 'F2L': 0.05, 'F3': 0.25, 'F4R': 0.03, 'F4L': 0.03, 'F5': 0.03, 'F6': 0.03}
 SENDS = {'F0': (0,), 'F1': (1, 2, 3, 4), 'F2R': (5,), 'F2L': (6,), 'F3': (7, 8), 'F4R': (9,), 'F4L': (10,), 'F5': (11,)}
 RECVS = {'F1': (0,), 'F2R': (1,), 'F2L': (2,), 'F3': (3, 4, 5, 6), 'F4R': (7,), 'F4L': (8,), 'F5': (9, 10), 'F6': (11,)}
 AFTER = {'F1': ('F0',), 'F2R': ('F1',), 'F2L': ('F1',), 'F3': ('F2R', 'F2L'), 'F4R': ('F3',), 'F4L': ('F3',),
          'F5': ('F4R', 'F4L'), 'F6': ('F5',)}
-SOURCE = ('G2', 'G4', 'ATO', 'ATG')
-NEEDS = {'G1': (), 'G2': ('G1',), 'G3': ('G1',), 'G4': ('G3',), 'ATF': (), 'ATO': ('ATF',), 'ATB': ('ATF',), 'ATG': ('ATB',)}
-RANK = ('G1', 'G2', 'ATF', 'ATO', 'ATB', 'ATG', 'G3', 'G4')
+MSG_US = ((1.5, 1.0),) + ((2.8, 1.9),) * 6 + ((5.6, 1.9),) * 2 + ((2.8, 1.9),) * 2 + ((1.5, 1.0),)
+RANK = ('G1', 'G2', 'ATF', 'ATO', 'ATB', 'ATG', 'G3', 'G4', 'PREP')
 
 
 def plan_order():
+    per = N_CHUNKS // N_GROUPS
     todo = {}
+
+    def add(key, needs, sends=()):
+        todo[key] = (needs, STEP_US[key[0]] if key[0] in STEP_US else SUM_US[key[0]], sends)
+
+    for g in range(N_GROUPS):
+        chunks = range(g * per, (g + 1) * per)
+        add(('G1', g), [])
+        add(('G2', g), [('G1', g)])
+        add(('ATF', g), [('F6', 0, c) for c in chunks] + [('PREP',)])
+        add(('ATO', g), [('ATF', g)])
+        add(('ATB', g), [('F6', 1, c) for c in chunks] + [('ATF', g)])
+        add(('ATG', g), [('ATB', g)])
+    for j in range(N_PARTS):
+        add(('G3', j), [('G1', g) for g in range(N_GROUPS)])
+        add(('G4', j), [('G3', k) for k in range(N_PARTS)])
+    add(('PREP',), [('G4', j) for j in range(N_PARTS)])
     for c in range(N_CHUNKS):
-        for name, pre in NEEDS.items():
-            needs = [(p, c) for p in pre]
-            if name in ('ATF', 'ATB'):
-                needs.append(('F6', int(name == 'ATB'), c))
-            todo[name, c] = (needs, STEP_US[name] / N_CHUNKS / 2, ())
+        g = c // per
+        source = ([('G2', g)], [('G4', j) for j in range(N_PARTS)], [('ATO', g)], [('ATG', g)])
         for a in range(N_SUMS):
-            for name, cost in SUM_US.items():
+            for name in SUM_US:
                 needs = [(p, a, c) for p in AFTER.get(name, ())] + [(i, a, c) for i in RECVS.get(name, ())]
-                if name == 'F0':
-                    needs.append((SOURCE[a], c))
-                todo[name, a, c] = (needs, cost, SENDS.get(name, ()))
+                add((name, a, c), needs + source[a] if name == 'F0' else needs, SENDS.get(name, ()))
 
     def rank(key):
         if key[0] in STEP_US:
             pos = RANK.index(key[0])
-            return (-1, key[1], pos) if pos < 2 else (1, pos, key[1])
+            return (-1, key[1], pos) if pos < 2 else (1, pos) + key[1:]
         return (0,) + key[1:] + (key[0],)
 
     now, order, done, free = LOAD_US, [], {}, {}
@@ -96,7 +108,7 @@
 def block_kernel(n_tp, head_dim, seq_len,
                  lens_ref, y1_hbm, y2_hbm, dy1_hbm, dy2_hbm, wq_hbm, wk_hbm, wv_hbm, wo_hbm, w1_hbm, w2_hbm,
                  x1_hbm, x2_hbm, dx1_hbm, dx2_hbm, ng_hbm, nf_hbm, act_hbm, dpre_hbm, attn_hbm, dqkv_hbm,
-                 w1, w2, wqkv, wo, y1, dy2, y2_own, dy1_own, ng, nf, act, dact, dpre, qkv, prob, attn, dqkv,
+                 w1, w2, wqkv, wo, wq_raw, wq_f, y1, dy2, dyb, y2_own, dy1_own, ng, nf, act, dact, dpre, qkv, prob, attn, dqkv,
                  part, d2d, ring1, ring2, full,
                  load_sem, out_sem, send_sem, recv_sem):
     tokens, width = y1.shape
@@ -136,36 +148,30 @@
 
     loads = {}
 
-    def load(name, src, dst):
-        loads[name] = pltpu.make_async_copy(src, dst, load_sem.at[len(loads)])
-        loads[name].start()
-
     def arrived(*names):
         for name in names:
             if name in loads:
                 loads.pop(name).wait()
 
     n_blk = ff // 256
-    waits = []
 
     def load_all():
-        c_rows = [pl.ds(c * chunk, chunk) for c in range(N_CHUNKS)]
-        load_list = [(('y1', 0), y1_hbm.at[c_rows[0]], y1.at[c_rows[0]])]
-        load_list += [(('w1', j), w1_hbm.at[:, pl.ds(j * 256, 256)], w1.at[:, pl.ds(j * 256, 256)]) for j in range(n_blk)]
-        load_list += [(('y1', c), y1_hbm.at[c_rows[c]], y1.at[c_rows[c]]) for c in range(1, N_CHUNKS)]
-        load_list += [(('w2',), w2_hbm, w2), (('dy2',), dy2_hbm, dy2)]
+        groups = [pl.ds(g * (tokens // N_GROUPS), tokens // N_GROUPS) for g in range(N_GROUPS)]
+        blocks = [pl.ds(j * 256, 256) for j in range(n_blk)]
+        todo = [(('y1', 0), y1_hbm.at[groups[0]], y1.at[groups[0]])]
+        todo += [(('w1', j), w1_hbm.at[:, blk], w1.at[:, blk]) for j, blk in enumerate(blocks)]
+        todo += [(('y1', g), y1_hbm.at[groups[g]], y1.at[groups[g]]) for g in range(1, N_GROUPS)]
+        todo += [(('w2',), w2_hbm, w2), (('dy2',), dy2_hbm, dy2)]
         for c in range(N_CHUNKS):
-            load_list += [(('y2o', c), y2_hbm.at[piece_rows(c, chip)], y2_own.at[own_rows(c)]),
-                          (('dy1o', c), dy1_hbm.at[piece_rows(c, chip)], dy1_own.at[own_rows(c)])]
-        kv = head_dim
-        load_list += [(('wqkv', 0), wq_hbm, wqkv.at[:, pl.ds(0, qdim)]),
-                      (('wqkv', 1), wk_hbm, wqkv.at[:, pl.ds(qdim, kv)]),
-                      (('wqkv', 2), wv_hbm, wqkv.at[:, pl.ds(qdim + kv, kv)]),
-                      (('wo',), wo_hbm, wo)]
-        for i, (name, src, dst) in enumerate(load_list):
-            copy = pltpu.make_async_copy(src, dst, load_sem.at[i])
-            copy.start()
-            loads[name] = copy
+            todo += [(('y2o', c), y2_hbm.at[piece_rows(c, chip)], y2_own.at[own_rows(c)]),
+                     (('dy1o', c), dy1_hbm.at[piece_rows(c, chip)], dy1_own.at[own_rows(c)])]
+        todo += [(('wq',), wq_hbm, wq_raw),
+                 (('wk',), wk_hbm, wqkv.at[:, pl.ds(qdim, head_dim)]),
+                 (('wv',), wv_hbm, wqkv.at[:, pl.ds(qdim + head_dim, head_dim)]),
+                 (('wo',), wo_hbm, wo)]
+        for i, (name, src, dst) in enumerate(todo):
+            loads[name] = pltpu.make_async_copy(src, dst, load_sem.at[i])
+            loads[name].start()
 
     outs = []
 
@@ -275,75 +281,66 @@
         rows = pl.ds(c * chunk, chunk)
         store(full.at[a, rows], (x2_hbm, dx1_hbm, x1_hbm, dx2_hbm)[a].at[rows])
 
-    def g1(c):
-        rows = pl.ds(c * chunk, chunk)
-        arrived(('y1', c))
+    group = tokens // N_GROUPS
+
+    def group_rows(g):
+        return pl.ds(g * group, group)
+
+    def g1(g):
+        rows = group_rows(g)
+        arrived(('y1', g))
         y_val = y1[rows]
         ng[rows] = (y_val * inv_rms(y_val)).astype(BF16)
         store(ng.at[rows], ng_hbm.at[rows])
-
-        def gelu_block(j):
-            cols = pl.ds(pl.multiple_of(j * 256, 256), 256)
+        for j in range(n_blk):
+            cols = pl.ds(j * 256, 256)
+            arrived(('w1', j))
             pre = mm(ng[rows], w1[:, cols])
-            inner = GELU_C * (pre + GELU_A * (pre * pre * pre))
-            th = jnp.tanh(inner)
+            th = jnp.tanh(GELU_C * (pre + GELU_A * (pre * pre * pre)))
             act[rows, cols] = (0.5 * pre * (1.0 + th)).astype(BF16)
             dact[rows, cols] = 0.5 * (1.0 + th) + (0.5 * pre) * (1.0 - th * th) * (
                 GELU_C * (1.0 + (3.0 * GELU_A) * (pre * pre)))
-
-        if c == 0:
-            for j in range(n_blk):
-                arrived(('w1', j))
-                gelu_block(j)
-        else:
-            pl.loop(0, n_blk)(gelu_block)
         store(act.at[rows], act_hbm.at[rows])
 
-    def g2(c):
-        rows = pl.ds(c * chunk, chunk)
+    def g2(g):
+        rows = group_rows(g)
         arrived(('w2',))
-
-        @pl.loop(0, width // 512)
-        def _(j):
-            cols = pl.ds(pl.multiple_of(j * 512, 512), 512)
-            part[0, rows, cols] = mm(act[rows], w2[:, cols])
-
-    def g3(c):
-        rows = pl.ds(c * chunk, chunk)
+        part[0, rows] = mm(act[rows], w2[...])
+
+    def g3(j):
         arrived(('dy2',))
-
-        @pl.loop(0, n_blk)
-        def _(j):
-            cols = pl.ds(pl.multiple_of(j * 256, 256), 256)
-            d_act = mm_nt(dy2[rows].astype(BF16), w2[cols])
-            dpre[rows, cols] = (dact[rows, cols] * d_act).astype(BF16)
-
-        store(dpre.at[rows], dpre_hbm.at[rows])
-
-    def g4(c):
-        rows = pl.ds(c * chunk, chunk)
-
-        @pl.loop(0, width // 256)
-        def _(j):
-            cols = pl.ds(pl.multiple_of(j * 256, 256), 256)
-            part[1, rows, cols] = mm_nt(dpre[rows], w1[cols])
-
-    def atf(c):
-        rows = pl.ds(c * chunk, chunk)
-        arrived(*(('wqkv', i) for i in range(3)))
+        cols = pl.ds(j * (ff // N_PARTS), ff // N_PARTS)
+        if j == 0:
+            dyb[...] = dy2[...].astype(BF16)
+        dpre[:, cols] = (dact[:, cols] * mm_nt(dyb[...], w2[cols])).astype(BF16)
+        store(dpre.at[:, cols], dpre_hbm.at[:, cols])
+
+    def g4(j):
+        cols = pl.ds(j * (width // N_PARTS), width // N_PARTS)
+        part[1, :, cols] = mm_nt(dpre[...], w1[cols])
+
+    def prep():
+        arrived(('wq',))
+        wq_f[...] = wq_raw[...].astype(F32)
+        for h in range(n_heads):
+            wqkv[:, pl.ds(h * head_dim, head_dim)] = wq_f[pl.ds(h, width, stride=n_heads)].astype(BF16)
+
+    def atf(g):
+        rows = group_rows(g)
+        arrived(('wk',), ('wv',))
         x_val = full[0, rows]
         nf[rows] = (x_val * inv_rms(x_val)).astype(BF16)
         store(nf.at[rows], nf_hbm.at[rows])
         qkv[rows] = mm(nf[rows], wqkv[...]).astype(BF16)
         key = qkv[rows, pl.ds(qdim, head_dim)]
         val = qkv[rows, pl.ds(qdim + head_dim, head_dim)]
-        n_seqs = chunk // seq_len
-        row_pos = lax.broadcasted_iota(jnp.int32, (chunk, chunk), 0)
-        col_pos = lax.broadcasted_iota(jnp.int32, (chunk, chunk), 1)
-        visible = jnp.zeros((chunk, chunk), jnp.bool_)
+        n_seqs = group // seq_len
+        row_pos = lax.broadcasted_iota(jnp.int32, (group, group), 0)
+        col_pos = lax.broadcasted_iota(jnp.int32, (group, group), 1)
+        visible = jnp.zeros((group, group), jnp.bool_)
         for s in range(n_seqs):
             base = s * seq_len
-            stop = base + lens_ref[c * n_seqs + s]
+            stop = base + lens_ref[g * n_seqs + s]
             visible = visible | ((row_pos >= base) & (row_pos < base + seq_len)
                                  & (col_pos >= base) & (col_pos < stop) & (col_pos <= row_pos))
         for h in range(n_heads):
@@ -356,22 +353,18 @@
             attn[rows, cols] = mm(probs.astype(BF16), val).astype(BF16)
         store(attn.at[rows], attn_hbm.at[rows])
 
-    def ato(c):
-        rows = pl.ds(c * chunk, chunk)
+    def ato(g):
+        rows = group_rows(g)
         arrived(('wo',))
-
-        @pl.loop(0, width // 512)
-        def _(j):
-            cols = pl.ds(pl.multiple_of(j * 512, 512), 512)
-            part[2, rows, cols] = mm(attn[rows], wo[:, cols])
-
-    def atb(c):
-        rows = pl.ds(c * chunk, chunk)
+        part[2, rows] = mm(attn[rows], wo[...])
+
+    def atb(g):
+        rows = group_rows(g)
         d_attn = mm_nt(full[1, rows].astype(BF16), wo[...]).astype(BF16)
         key = qkv[rows, pl.ds(qdim, head_dim)]
         val = qkv[rows, pl.ds(qdim + head_dim, head_dim)]
-        d_key = jnp.zeros((chunk, head_dim), F32)
-        d_val = jnp.zeros((chunk, head_dim), F32)
+        d_key = jnp.zeros((group, head_dim), F32)
+        d_val = jnp.zeros((group, head_dim), F32)
         for h in range(n_heads):
             cols = pl.ds(h * head_dim, head_dim)
             d_head = d_attn[:, h * head_dim:(h + 1) * head_dim]
@@ -386,16 +379,12 @@
         dqkv[rows, pl.ds(qdim + head_dim, head_dim)] = d_val.astype(BF16)
         store(dqkv.at[rows], dqkv_hbm.at[rows])
 
-    def atg(c):
-        rows = pl.ds(c * chunk, chunk)
-
-        @pl.loop(0, width // 256)
-        def _(j):
-            cols = pl.ds(pl.multiple_of(j * 256, 256), 256)
-            part[3, rows, cols] = mm_nt(dqkv[rows], wqkv[cols])
+    def atg(g):
+        rows = group_rows(g)
+        part[3, rows] = mm_nt(dqkv[rows], wqkv[...])
 
     steps = {'F0': f0, 'F1': f1, 'F2R': f2r, 'F2L': f2l, 'F3': f3, 'F4R': f4r, 'F4L': f4l, 'F5': f5, 'F6': f6,
-             'G1': g1, 'G2': g2, 'G3': g3, 'G4': g4, 'ATF': atf, 'ATO': ato, 'ATB': atb, 'ATG': atg}
+             'G1': g1, 'G2': g2, 'G3': g3, 'G4': g4, 'PREP': prep, 'ATF': atf, 'ATO': ato, 'ATB': atb, 'ATG': atg}
     load_all()
     for name, *where in plan_order():
         steps[name](*where)
@@ -414,12 +403,11 @@
     ff = w_up.shape[1]
     qdim = n_heads * head_dim
     qkv_dim = qdim + 2 * head_dim
-    chunk = tokens // N_CHUNKS
     units = N_SUMS * N_CHUNKS
-    half = chunk // 2
+    half = tokens // N_CHUNKS // 2
     piece = half // (n_tp // 2)
     acts = tuple(v.reshape(tokens, width) for v in (y_one, y_two, dy_one, dy_two))
-    weights = (w_query.reshape(width, qdim), w_key.reshape(width, head_dim), w_value.reshape(width, head_dim),
+    weights = (w_query.reshape(width * n_heads, head_dim), w_key.reshape(width, head_dim), w_value.reshape(width, head_dim),
                w_out.reshape(qdim, width), w_up, w_down)
     sds = jax.ShapeDtypeStruct
     out_shape = [sds((tokens, width), F32)] * 4 + [
@@ -428,11 +416,12 @@
     vm = pltpu.VMEM
     scratch = [
         vm((width, ff), BF16), vm((ff, width), BF16), vm((width, qkv_dim), BF16), vm((qdim, width), BF16),
-        vm((tokens, width), F32), vm((tokens, width), F32),
+        vm((width * n_heads, head_dim), BF16), vm((width * n_heads, head_dim), F32),
+        vm((tokens, width), F32), vm((tokens, width), F32), vm((tokens, width), BF16),
         vm((N_CHUNKS * piece, width), F32), vm((N_CHUNKS * piece, width), F32),
         vm((tokens, width), BF16), vm((tokens, width), BF16),
         vm((tokens, ff), BF16), vm((tokens, ff), F32), vm((tokens, ff), BF16),
-        vm((tokens, qkv_dim), BF16), vm((n_heads, tokens, chunk), F32), vm((tokens, qdim), BF16),
+        vm((tokens, qkv_dim), BF16), vm((n_heads, tokens, tokens // N_GROUPS), F32), vm((tokens, qdim), BF16),
         vm((tokens, qkv_dim), BF16),
         vm((N_SUMS, tokens, width), F32), vm((units * half, width), F32),
         vm((2, units * piece, width // 2), F32), vm((2, units * piece, width), F32),
@@ -453,16 +442,92 @@
     )(seq_lens, *acts, *weights)
 
 
-def weight_grads(dy_two, dx1, ng, nf, act, dpre, attn, dqkv, n_heads, head_dim):
-    qdim = n_heads * head_dim
-    e_val, c_val = dy_two.astype(BF16), dx1.astype(BF16)
-    dw_down = mm_tn(act, e_val)
-    dw_up = mm_tn(ng, dpre)
-    dw_out = mm_tn(attn, c_val)
-    dw_query = mm_tn(nf, dqkv[:, :qdim])
-    dw_key = mm_tn(nf, dqkv[:, qdim:qdim + head_dim])
-    dw_value = mm_tn(nf, dqkv[:, qdim + head_dim:])
-    return dw_query, dw_key, dw_value, dw_out, dw_up, dw_down
+def grads_kernel(head_dim, n_blk,
+                 x1_in, x2_in, dx1_in, dx2_in, dy2_in, ng_in, nf_in, act_in, dpre_in, attn_in, dqkv_in,
+                 x1_out, x2_out, dx1_out, dx2_out, dwq_out, dwk_out, dwv_out, dwo_out, dw1_out, dw2_out,
+                 state, dy2, ng, nf, act, dpre, attn, dqkv, e_val, c_val, dwq, dwk, dwv, dwo, dw1, dw2,
+                 in_sem, out_sem):
+    ins = {}
+    todo = [('act', act_in, act), ('dy2', dy2_in, dy2), ('ng', ng_in, ng), ('dpre', dpre_in, dpre),
+            ('dx1', dx1_in, state.at[2]), ('attn', attn_in, attn), ('nf', nf_in, nf), ('dqkv', dqkv_in, dqkv),
+            ('x1', x1_in, state.at[0]), ('x2', x2_in, state.at[1]), ('dx2', dx2_in, state.at[3])]
+    for i, (name, src, dst) in enumerate(todo):
+        ins[name] = pltpu.make_async_copy(src, dst, in_sem.at[i])
+        ins[name].start()
+
+    def arrived(*names):
+        for name in names:
+            if name in ins:
+                ins.pop(name).wait()
+
+    outs = []
+
+    def store(src, dst):
+        outs.append(pltpu.make_async_copy(src, dst, out_sem.at[len(outs)]))
+        outs[-1].start()
+
+    width, ff = dw1.shape
+    qdim = attn.shape[1]
+    n_heads = qdim // head_dim
+    arrived('act', 'dy2')
+    e_val[...] = dy2[...].astype(BF16)
+    rows2, rows1 = ff // n_blk, width // n_blk
+    for j in range(n_blk):
+        rows = pl.ds(j * rows2, rows2)
+        dw2[rows] = mm_tn(act[:, rows], e_val[...])
+        store(dw2.at[rows], dw2_out.at[rows])
+    arrived('ng', 'dpre')
+    for j in range(n_blk):
+        rows = pl.ds(j * rows1, rows1)
+        dw1[rows] = mm_tn(ng[:, rows], dpre[...])
+        store(dw1.at[rows], dw1_out.at[rows])
+    arrived('dx1', 'attn')
+    c_val[...] = state[2].astype(BF16)
+    store(state.at[2], dx1_out)
+    for h in range(n_heads):
+        rows = pl.ds(h * head_dim, head_dim)
+        dwo[rows] = mm_tn(attn[:, rows], c_val[...])
+        store(dwo.at[rows], dwo_out.at[rows])
+    for name, i, out in (('x1', 0, x1_out), ('x2', 1, x2_out), ('dx2', 3, dx2_out)):
+        arrived(name)
+        store(state.at[i], out)
+    arrived('nf', 'dqkv')
+    for j in range(n_blk // 2):
+        step = width // (n_blk // 2)
+        rows = pl.ds(j * step, step)
+        grad = mm_tn(nf[:, rows], dqkv[...])
+        for h in range(n_heads):
+            dwq[pl.ds(j * step * n_heads + h, step, stride=n_heads)] = grad[:, h * head_dim:(h + 1) * head_dim]
+        dwk[rows] = grad[:, qdim:qdim + head_dim]
+        dwv[rows] = grad[:, qdim + head_dim:]
+        rows_q = pl.ds(j * step * n_heads, step * n_heads)
+        store(dwq.at[rows_q], dwq_out.at[rows_q])
+        store(dwk.at[rows], dwk_out.at[rows])
+        store(dwv.at[rows], dwv_out.at[rows])
+    for copy in outs:
+        copy.wait()
+
+
+def grads_call(dy_two, x1, x2, dx1, dx2, ng, nf, act, dpre, attn, dqkv, n_heads, head_dim):
+    tokens, width = x1.shape
+    ff, qdim, qkv_dim = act.shape[1], attn.shape[1], dqkv.shape[1]
+    sds, vm = jax.ShapeDtypeStruct, pltpu.VMEM
+    dw_shapes = [(width * n_heads, head_dim), (width, head_dim), (width, head_dim), (qdim, width), (width, ff), (ff, width)]
+    scratch = [vm((4, tokens, width), F32), vm((tokens, width), F32), vm((tokens, width), BF16), vm((tokens, width), BF16),
+               vm((tokens, ff), BF16), vm((tokens, ff), BF16), vm((tokens, qdim), BF16), vm((tokens, qkv_dim), BF16),
+               vm((tokens, width), BF16), vm((tokens, width), BF16)]
+    scratch += [vm(s, F32) for s in dw_shapes]
+    scratch += [pltpu.SemaphoreType.DMA((16,)), pltpu.SemaphoreType.DMA((48,))]
+    return pl.pallas_call(
+        functools.partial(grads_kernel, head_dim, 8),
+        out_shape=[sds((tokens, width), F32)] * 4 + [sds(s, F32) for s in dw_shapes],
+        in_specs=[ANY] * 11,
+        out_specs=[ANY] * 10,
+        scratch_shapes=scratch,
+        name='weight_grads',
+        compiler_params=pltpu.CompilerParams(vmem_limit_bytes=60 * 1024 * 1024),
+        cost_estimate=pl.CostEstimate(flops=4 * 10 ** 9, bytes_accessed=4 * 10 ** 7, transcendentals=0),
+    )(x1, x2, dx1, dx2, dy_two, ng, nf, act, dpre, attn, dqkv)
 
 
 def solution(mesh):
@@ -477,11 +542,10 @@
         n_heads, head_dim = w_query.shape[2], w_query.shape[3]
         tokens, width = y_one.shape[0] * y_one.shape[1], y_one.shape[2]
         ws = tuple(w[0] for w in (w_query, w_key, w_value, w_out, w_up, w_down))
-        x1, x2, dx1, dx2, ng, nf, act, dpre, attn, dqkv = block_call(
-            n_tp, seq_lens, y_one, y_two, dy_one, dy_two, *ws)
-        dw = weight_grads(dy_two.reshape(tokens, width), dx1, ng, nf, act, dpre, attn, dqkv, n_heads, head_dim)
-        dw = tuple(g.reshape((1,) + w.shape) for g, w in zip(dw, ws))
-        return tuple(v.reshape(y_one.shape) for v in (x1, x2, dx1, dx2)) + dw
+        saved = block_call(n_tp, seq_lens, y_one, y_two, dy_one, dy_two, *ws)
+        res = grads_call(dy_two.reshape(tokens, width), *saved, n_heads, head_dim)
+        dw = tuple(g.reshape((1,) + w.shape) for g, w in zip(res[4:], ws))
+        return tuple(v.reshape(y_one.shape) for v in res[:4]) + dw
 
     return jax.shard_map(local_fn, mesh=mesh,
                          in_specs=(act_spec,) * 4 + (P('dp'),) + w_specs,

time: 144 us -> 109 us (0.76)
  matrix products: 17.2 us -> 0 us
  local copies, waits for them, and re-layouts: 14 us -> 0 us
  Pallas kernels: 112 us -> 108 us
    pallas_call x1, Pallas kernels: 112 us -> 93.1 us  [block_call(): pl.pallas_call(functools.partial(block_kernel, n_tp, head_dim, seq_len),...]
    dot_general x6 -> x0, matrix products: 17.2 us -> none  [mm_tn(): lax.dot_general(lhs, rhs, (((0,), (0,)), ((), ())), preferred_element_typ...]
    pallas_call x0 -> x1, Pallas kernels: none -> 14.7 us  [grads_call(): pl.pallas_call(functools.partial(grads_kernel, head_dim, 8), out_shape=[s...]
    unnamed x28 -> x0, local copies, waits for them, and re-layouts: 14 us -> none
where the time goes in v2:
time: 109 us
  Pallas kernels  108 us (99%)
    pallas_call x1, Pallas kernels, block_call(): pl.pallas_call(functools.partial(block_kernel, n_tp, head_dim, seq_len),...  93.1 us
    pallas_call x1, Pallas kernels, grads_call(): pl.pallas_call(functools.partial(grads_kernel, head_dim, 8), out_shape=[s...  14.7 us

profile of v2, /device:TPU:81, one launch (start us, length us, event | category | flops | bytes accessed | tf_op | source)
XLA Modules:
  0.0 108.5 jit_solution(12279595304218194900)
XLA Ops:
  0.6 93.1 %block_back.1 = (f32[256,2048]{1,0:T(8,128)}, f32[256,2048]{1,0:T(8,128)}, f32[256,2048]{1,0:T(8,128)}, f32[256,2048]{1,0:T(8,128)}, bf16[256,2048]{1,0:T(8,128)...) custom-call(s32[8]{0:T(128)} %lens_ref.1, ...), custom_call_target="tpu_custom_call" | custom-call | flops 10000000000 | bytes 30000000 | tf_op jit(solution)/shard_map/block_back/pallas_call | solution.py:432
  93.7 14.7 %weight_grads.1 = (f32[256,2048]{1,0:T(8,128)}, f32[256,2048]{1,0:T(8,128)}, f32[256,2048]{1,0:T(8,128)}, f32[256,2048]{1,0:T(8,128)}, f32[4096,128]{1,0:T(8,128...) custom-call(f32[256,2048]{1,0:T(8,128)} %get-tuple-element.30.x1_in,, ...), custom_call_target="tpu_custom_call" | custom-call | flops 4000000000 | bytes 40000000 | tf_op jit(solution)/shard_map/weight_grads/pallas_call | solution.py:521

commit v3 on v2

--- a/solution.py
+++ b/solution.py
@@ -20,6 +20,7 @@
 N_PARTS = 2
 N_SUMS = 4
 N_MSGS = 12
+RECV_SLOT = (0, 1, 2, 3, 3, 3, 3, 4, 5, 6, 6, 7)
 
 LOAD_US = 3.5
 STEP_US = {'G1': 1.0, 'G2': 0.9, 'G3': 0.9, 'G4': 0.6, 'PREP': 1.0, 'ATF': 1.6, 'ATO': 0.6, 'ATB': 2.0, 'ATG': 1.2}
@@ -107,10 +108,11 @@
 
 def block_kernel(n_tp, head_dim, seq_len,
                  lens_ref, y1_hbm, y2_hbm, dy1_hbm, dy2_hbm, wq_hbm, wk_hbm, wv_hbm, wo_hbm, w1_hbm, w2_hbm,
-                 x1_hbm, x2_hbm, dx1_hbm, dx2_hbm, ng_hbm, nf_hbm, act_hbm, dpre_hbm, attn_hbm, dqkv_hbm,
-                 w1, w2, wqkv, wo, wq_raw, wq_f, y1, dy2, dyb, y2_own, dy1_own, ng, nf, act, dact, dpre, qkv, prob, attn, dqkv,
-                 part, d2d, ring1, ring2, full,
-                 load_sem, out_sem, send_sem, recv_sem):
+                 x2, dx1, x1, dx2, ng, nf, act, dpre, attn, dqkv, dyb,
+                 w1, w2, wqkv, wo, wq_raw, wq_f, y1, dy2, y2_own, dy1_own, dact, qkv, prob,
+                 part, d2d, ring1, ring2,
+                 load_sem, send_sem, recv_sem):
+    full = (x2, dx1, x1, dx2)
     tokens, width = y1.shape
     ff = w1.shape[1]
     qdim = attn.shape[1]
@@ -162,9 +164,6 @@
         todo += [(('w1', j), w1_hbm.at[:, blk], w1.at[:, blk]) for j, blk in enumerate(blocks)]
         todo += [(('y1', g), y1_hbm.at[groups[g]], y1.at[groups[g]]) for g in range(1, N_GROUPS)]
         todo += [(('w2',), w2_hbm, w2), (('dy2',), dy2_hbm, dy2)]
-        for c in range(N_CHUNKS):
-            todo += [(('y2o', c), y2_hbm.at[piece_rows(c, chip)], y2_own.at[own_rows(c)]),
-                     (('dy1o', c), dy1_hbm.at[piece_rows(c, chip)], dy1_own.at[own_rows(c)])]
         todo += [(('wq',), wq_hbm, wq_raw),
                  (('wk',), wk_hbm, wqkv.at[:, pl.ds(qdim, head_dim)]),
                  (('wv',), wv_hbm, wqkv.at[:, pl.ds(qdim + head_dim, head_dim)]),
@@ -172,19 +171,20 @@
         for i, (name, src, dst) in enumerate(todo):
             loads[name] = pltpu.make_async_copy(src, dst, load_sem.at[i])
             loads[name].start()
-
-    outs = []
-
-    def store(src, dst):
-        copy = pltpu.make_async_copy(src, dst, out_sem.at[len(outs)])
-        copy.start()
-        outs.append(copy)
+            if name == ('dy2',):
+                for k, src_hbm, own in ((14, y2_hbm, y2_own), (15, dy1_hbm, dy1_own)):
+                    for c in range(N_CHUNKS):
+                        pltpu.make_async_copy(src_hbm.at[piece_rows(c, chip)], own.at[own_rows(c)], load_sem.at[k]).start()
+                    loads['own', k] = pltpu.make_async_copy(own, own, load_sem.at[k])
+
+    def shared(a, c):
+        return a % 2 * N_CHUNKS + c
 
     def msg(a, c, i):
         rows_own, rows_r, rows_l, rows_o = (piece_rows(c, x) for x in (chip, chip_r, chip_l, chip_o))
         u = a * N_CHUNKS + c
         slot = pl.ds(u * piece, piece)
-        pa, oa = part.at[a], full.at[a]
+        pa, oa = part.at[a], full[a]
         if i == 0:
             src, dst, dev = pa.at[half_rows(c, 1 - core)], d2d.at[pl.ds(u * half, half)], partner
         elif i == 1:
@@ -209,16 +209,20 @@
             src, dst, dev = oa.at[rows_r, hi], oa.at[rows_r, hi], left
         else:
             src, dst, dev = oa.at[half_rows(c, core)], oa.at[half_rows(c, core)], partner
-        return pltpu.make_async_remote_copy(src, dst, send_sem.at[i, u], recv_sem.at[i, u],
+        return pltpu.make_async_remote_copy(src, dst, send_sem.at[i], recv_sem.at[RECV_SLOT[i], shared(a, c)],
                                             device_id={'tp': dev}, device_id_type=MESH)
 
     def send(a, c, *ids):
         for i in ids:
             msg(a, c, i).start()
 
-    def recv(a, c, *ids):
-        for i in ids:
-            msg(a, c, i).wait_recv()
+    def recv(a, c, *slots):
+        u = pl.ds((a * N_CHUNKS + c) * piece, piece)
+        own = full[a].at[piece_rows(c, chip)]
+        whole = (d2d.at[pl.ds((a * N_CHUNKS + c) * half, half)], ring1.at[0, u], ring1.at[1, u], ring2.at[:, u],
+                 own, own, own, full[a].at[half_rows(c, core)])
+        for s in slots:
+            pltpu.make_async_copy(whole[s], whole[s], recv_sem.at[s, shared(a, c)]).wait()
 
     state = {'met': False}
 
@@ -247,39 +251,37 @@
         send(a, c, 6)
 
     def f3(a, c):
-        recv(a, c, 3, 4, 5, 6)
+        recv(a, c, 3)
         rows = piece_rows(c, chip)
         slot = pl.ds((a * N_CHUNKS + c) * piece, piece)
         total = part[a, rows] + ring2[0, slot] + ring2[1, slot]
         if a == 0:
-            arrived(('y2o', c))
+            arrived(('own', 14))
             out = y2_own[own_rows(c)] - total
         elif a == 1:
-            arrived(('dy1o', c))
+            arrived(('own', 15))
             out = dy1_own[own_rows(c)] + rms_back(y1[rows], total)
         elif a == 2:
             out = y1[rows] - total
         else:
-            out = dy2[rows] + rms_back(full[0, rows], total)
-        full[a, rows] = out
+            out = dy2[rows] + rms_back(x2[rows], total)
+        full[a][rows] = out
         send(a, c, 7, 8)
 
     def f4r(a, c):
+        recv(a, c, 4)
+        send(a, c, 9)
+
+    def f4l(a, c):
+        recv(a, c, 5)
+        send(a, c, 10)
+
+    def f5(a, c):
+        recv(a, c, 6)
+        send(a, c, 11)
+
+    def f6(a, c):
         recv(a, c, 7)
-        send(a, c, 9)
-
-    def f4l(a, c):
-        recv(a, c, 8)
-        send(a, c, 10)
-
-    def f5(a, c):
-        recv(a, c, 9, 10)
-        send(a, c, 11)
-
-    def f6(a, c):
-        recv(a, c, 11)
-        rows = pl.ds(c * chunk, chunk)
-        store(full.at[a, rows], (x2_hbm, dx1_hbm, x1_hbm, dx2_hbm)[a].at[rows])
 
     group = tokens // N_GROUPS
 
@@ -291,7 +293,6 @@
         arrived(('y1', g))
         y_val = y1[rows]
         ng[rows] = (y_val * inv_rms(y_val)).astype(BF16)
-        store(ng.at[rows], ng_hbm.at[rows])
         for j in range(n_blk):
             cols = pl.ds(j * 256, 256)
             arrived(('w1', j))
@@ -300,7 +301,6 @@
             act[rows, cols] = (0.5 * pre * (1.0 + th)).astype(BF16)
             dact[rows, cols] = 0.5 * (1.0 + th) + (0.5 * pre) * (1.0 - th * th) * (
                 GELU_C * (1.0 + (3.0 * GELU_A) * (pre * pre)))
-        store(act.at[rows], act_hbm.at[rows])
 
     def g2(g):
         rows = group_rows(g)
@@ -313,7 +313,6 @@
         if j == 0:
             dyb[...] = dy2[...].astype(BF16)
         dpre[:, cols] = (dact[:, cols] * mm_nt(dyb[...], w2[cols])).astype(BF16)
-        store(dpre.at[:, cols], dpre_hbm.at[:, cols])
 
     def g4(j):
         cols = pl.ds(j * (width // N_PARTS), width // N_PARTS)
@@ -328,9 +327,8 @@
     def atf(g):
         rows = group_rows(g)
         arrived(('wk',), ('wv',))
-        x_val = full[0, rows]
+        x_val = x2[rows]
         nf[rows] = (x_val * inv_rms(x_val)).astype(BF16)
-        store(nf.at[rows], nf_hbm.at[rows])
         qkv[rows] = mm(nf[rows], wqkv[...]).astype(BF16)
         key = qkv[rows, pl.ds(qdim, head_dim)]
         val = qkv[rows, pl.ds(qdim + head_dim, head_dim)]
@@ -351,7 +349,6 @@
             probs = exps / jnp.sum(exps, axis=-1, keepdims=True)
             prob[h, rows] = probs
             attn[rows, cols] = mm(probs.astype(BF16), val).astype(BF16)
-        store(attn.at[rows], attn_hbm.at[rows])
 
     def ato(g):
         rows = group_rows(g)
@@ -360,7 +357,7 @@
 
     def atb(g):
         rows = group_rows(g)
-        d_attn = mm_nt(full[1, rows].astype(BF16), wo[...]).astype(BF16)
+        d_attn = mm_nt(dx1[rows].astype(BF16), wo[...]).astype(BF16)
         key = qkv[rows, pl.ds(qdim, head_dim)]
         val = qkv[rows, pl.ds(qdim + head_dim, head_dim)]
         d_key = jnp.zeros((group, head_dim), F32)
@@ -377,7 +374,6 @@
             d_val = d_val + mm_tn(probs.astype(BF16), d_head)
         dqkv[rows, pl.ds(qdim, head_dim)] = d_key.astype(BF16)
         dqkv[rows, pl.ds(qdim + head_dim, head_dim)] = d_val.astype(BF16)
-        store(dqkv.at[rows], dqkv_hbm.at[rows])
 
     def atg(g):
         rows = group_rows(g)
@@ -388,12 +384,9 @@
     load_all()
     for name, *where in plan_order():
         steps[name](*where)
-    for copy in outs:
-        copy.wait()
-    for a in range(N_SUMS):
-        for c in range(N_CHUNKS):
-            for i in range(N_MSGS):
-                msg(a, c, i).wait_send()
+    sent = (d2d,) + (ring1.at[0],) * 6 + (ring2.at[0],) * 2 + (ring1.at[0],) * 2 + (d2d,)
+    for i in range(N_MSGS):
+        pltpu.make_async_copy(sent[i], sent[i], send_sem.at[i]).wait()
 
 
 def block_call(n_tp, seq_lens, y_one, y_two, dy_one, dy_two, w_query, w_key, w_value, w_out, w_up, w_down):
@@ -409,89 +402,64 @@
     acts = tuple(v.reshape(tokens, width) for v in (y_one, y_two, dy_one, dy_two))
     weights = (w_query.reshape(width * n_heads, head_dim), w_key.reshape(width, head_dim), w_value.reshape(width, head_dim),
                w_out.reshape(qdim, width), w_up, w_down)
-    sds = jax.ShapeDtypeStruct
-    out_shape = [sds((tokens, width), F32)] * 4 + [
-        sds((tokens, width), BF16), sds((tokens, width), BF16), sds((tokens, ff), BF16), sds((tokens, ff), BF16),
-        sds((tokens, qdim), BF16), sds((tokens, qkv_dim), BF16)]
     vm = pltpu.VMEM
+    out_shape = [vm((tokens, width), F32)] * 4 + [
+        vm((tokens, width), BF16), vm((tokens, width), BF16), vm((tokens, ff), BF16), vm((tokens, ff), BF16),
+        vm((tokens, qdim), BF16), vm((tokens, qkv_dim), BF16), vm((tokens, width), BF16)]
     scratch = [
         vm((width, ff), BF16), vm((ff, width), BF16), vm((width, qkv_dim), BF16), vm((qdim, width), BF16),
         vm((width * n_heads, head_dim), BF16), vm((width * n_heads, head_dim), F32),
-        vm((tokens, width), F32), vm((tokens, width), F32), vm((tokens, width), BF16),
+        vm((tokens, width), F32), vm((tokens, width), F32),
         vm((N_CHUNKS * piece, width), F32), vm((N_CHUNKS * piece, width), F32),
-        vm((tokens, width), BF16), vm((tokens, width), BF16),
-        vm((tokens, ff), BF16), vm((tokens, ff), F32), vm((tokens, ff), BF16),
-        vm((tokens, qkv_dim), BF16), vm((n_heads, tokens, tokens // N_GROUPS), F32), vm((tokens, qdim), BF16),
-        vm((tokens, qkv_dim), BF16),
+        vm((tokens, ff), F32), vm((tokens, qkv_dim), BF16), vm((n_heads, tokens, tokens // N_GROUPS), F32),
         vm((N_SUMS, tokens, width), F32), vm((units * half, width), F32),
         vm((2, units * piece, width // 2), F32), vm((2, units * piece, width), F32),
-        vm((N_SUMS, tokens, width), F32),
-        pltpu.SemaphoreType.DMA((32,)), pltpu.SemaphoreType.DMA((48,)),
-        pltpu.SemaphoreType.DMA((N_MSGS, units)), pltpu.SemaphoreType.DMA((N_MSGS, units)),
+        pltpu.SemaphoreType.DMA((16,)), pltpu.SemaphoreType.DMA((N_MSGS,)), pltpu.SemaphoreType.DMA((8, units // 2)),
     ]
     return pl.pallas_call(
         functools.partial(block_kernel, n_tp, head_dim, seq_len),
         out_shape=out_shape,
         in_specs=[pl.BlockSpec(memory_space=pltpu.SMEM)] + [ANY] * 10,
-        out_specs=[ANY] * len(out_shape),
+        out_specs=[pl.BlockSpec(memory_space=pltpu.VMEM)] * len(out_shape),
         scratch_shapes=scratch,
         name='block_back',
         compiler_params=pltpu.CompilerParams(collective_id=0, has_side_effects=True,
-                                             vmem_limit_bytes=60 * 1024 * 1024),
+                                             vmem_limit_bytes=46 * 1024 * 1024),
         cost_estimate=pl.CostEstimate(flops=10 ** 10, bytes_accessed=3 * 10 ** 7, transcendentals=10 ** 6),
     )(seq_lens, *acts, *weights)
 
 
 def grads_kernel(head_dim, n_blk,
-                 x1_in, x2_in, dx1_in, dx2_in, dy2_in, ng_in, nf_in, act_in, dpre_in, attn_in, dqkv_in,
-                 x1_out, x2_out, dx1_out, dx2_out, dwq_out, dwk_out, dwv_out, dwo_out, dw1_out, dw2_out,
-                 state, dy2, ng, nf, act, dpre, attn, dqkv, e_val, c_val, dwq, dwk, dwv, dwo, dw1, dw2,
-                 in_sem, out_sem):
-    ins = {}
-    todo = [('act', act_in, act), ('dy2', dy2_in, dy2), ('ng', ng_in, ng), ('dpre', dpre_in, dpre),
-            ('dx1', dx1_in, state.at[2]), ('attn', attn_in, attn), ('nf', nf_in, nf), ('dqkv', dqkv_in, dqkv),
-            ('x1', x1_in, state.at[0]), ('x2', x2_in, state.at[1]), ('dx2', dx2_in, state.at[3])]
-    for i, (name, src, dst) in enumerate(todo):
-        ins[name] = pltpu.make_async_copy(src, dst, in_sem.at[i])
-        ins[name].start()
-
-    def arrived(*names):
-        for name in names:
-            if name in ins:
-                ins.pop(name).wait()
-
+                 x2, dx1, x1, dx2, ng, nf, act, dpre, attn, dqkv, e_val,
+                 x2_out, dx1_out, x1_out, dx2_out, dwq_out, dwk_out, dwv_out, dwo_out, dw1_out, dw2_out,
+                 c_val, dwq, dwk, dwv, dwo, dw1, dw2, out_sem):
     outs = []
 
     def store(src, dst):
         outs.append(pltpu.make_async_copy(src, dst, out_sem.at[len(outs)]))
         outs[-1].start()
 
+    store(x2, x2_out)
+    store(dx1, dx1_out)
     width, ff = dw1.shape
     qdim = attn.shape[1]
     n_heads = qdim // head_dim
-    arrived('act', 'dy2')
-    e_val[...] = dy2[...].astype(BF16)
     rows2, rows1 = ff // n_blk, width // n_blk
     for j in range(n_blk):
         rows = pl.ds(j * rows2, rows2)
         dw2[rows] = mm_tn(act[:, rows], e_val[...])
         store(dw2.at[rows], dw2_out.at[rows])
-    arrived('ng', 'dpre')
     for j in range(n_blk):
         rows = pl.ds(j * rows1, rows1)
         dw1[rows] = mm_tn(ng[:, rows], dpre[...])
         store(dw1.at[rows], dw1_out.at[rows])
-    arrived('dx1', 'attn')
-    c_val[...] = state[2].astype(BF16)
-    store(state.at[2], dx1_out)
+    store(x1, x1_out)
+    store(dx2, dx2_out)
+    c_val[...] = dx1[...].astype(BF16)
     for h in range(n_heads):
         rows = pl.ds(h * head_dim, head_dim)
         dwo[rows] = mm_tn(attn[:, rows], c_val[...])
         store(dwo.at[rows], dwo_out.at[rows])
-    for name, i, out in (('x1', 0, x1_out), ('x2', 1, x2_out), ('dx2', 3, dx2_out)):
-        arrived(name)
-        store(state.at[i], out)
-    arrived('nf', 'dqkv')
     for j in range(n_blk // 2):
         step = width // (n_blk // 2)
         rows = pl.ds(j * step, step)
@@ -508,26 +476,22 @@
         copy.wait()
 
 
-def grads_call(dy_two, x1, x2, dx1, dx2, ng, nf, act, dpre, attn, dqkv, n_heads, head_dim):
-    tokens, width = x1.shape
-    ff, qdim, qkv_dim = act.shape[1], attn.shape[1], dqkv.shape[1]
+def grads_call(n_heads, head_dim, *saved):
+    tokens, width = saved[0].shape
+    ff, qdim = saved[6].shape[1], n_heads * head_dim
     sds, vm = jax.ShapeDtypeStruct, pltpu.VMEM
     dw_shapes = [(width * n_heads, head_dim), (width, head_dim), (width, head_dim), (qdim, width), (width, ff), (ff, width)]
-    scratch = [vm((4, tokens, width), F32), vm((tokens, width), F32), vm((tokens, width), BF16), vm((tokens, width), BF16),
-               vm((tokens, ff), BF16), vm((tokens, ff), BF16), vm((tokens, qdim), BF16), vm((tokens, qkv_dim), BF16),
-               vm((tokens, width), BF16), vm((tokens, width), BF16)]
-    scratch += [vm(s, F32) for s in dw_shapes]
-    scratch += [pltpu.SemaphoreType.DMA((16,)), pltpu.SemaphoreType.DMA((48,))]
+    scratch = [vm((tokens, width), BF16)] + [vm(s, F32) for s in dw_shapes] + [pltpu.SemaphoreType.DMA((40,))]
     return pl.pallas_call(
         functools.partial(grads_kernel, head_dim, 8),
         out_shape=[sds((tokens, width), F32)] * 4 + [sds(s, F32) for s in dw_shapes],
-        in_specs=[ANY] * 11,
+        in_specs=[pl.BlockSpec(memory_space=pltpu.VMEM)] * len(saved),
         out_specs=[ANY] * 10,
         scratch_shapes=scratch,
         name='weight_grads',
-        compiler_params=pltpu.CompilerParams(vmem_limit_bytes=60 * 1024 * 1024),
+        compiler_params=pltpu.CompilerParams(vmem_limit_bytes=34 * 1024 * 1024),
         cost_estimate=pl.CostEstimate(flops=4 * 10 ** 9, bytes_accessed=4 * 10 ** 7, transcendentals=0),
-    )(x1, x2, dx1, dx2, dy_two, ng, nf, act, dpre, attn, dqkv)
+    )(*saved)
 
 
 def solution(mesh):
@@ -540,12 +504,11 @@
 
     def local_fn(y_one, y_two, dy_one, dy_two, seq_lens, w_query, w_key, w_value, w_out, w_up, w_down):
         n_heads, head_dim = w_query.shape[2], w_query.shape[3]
-        tokens, width = y_one.shape[0] * y_one.shape[1], y_one.shape[2]
         ws = tuple(w[0] for w in (w_query, w_key, w_value, w_out, w_up, w_down))
         saved = block_call(n_tp, seq_lens, y_one, y_two, dy_one, dy_two, *ws)
-        res = grads_call(dy_two.reshape(tokens, width), *saved, n_heads, head_dim)
+        res = grads_call(n_heads, head_dim, *saved)
         dw = tuple(g.reshape((1,) + w.shape) for g, w in zip(res[4:], ws))
-        return tuple(v.reshape(y_one.shape) for v in res[:4]) + dw
+        return tuple(v.reshape(y_one.shape) for v in (res[2], res[0], res[1], res[3])) + dw
 
     return jax.shard_map(local_fn, mesh=mesh,
                          in_specs=(act_spec,) * 4 + (P('dp'),) + w_specs,

time: 109 us -> 99.9 us (0.917)
  Pallas kernels: 108 us -> 99 us
    pallas_call x1, Pallas kernels: 93.1 us -> 88.5 us  [block_call(): pl.pallas_call(functools.partial(block_kernel, n_tp, head_dim, seq_len),...]
    pallas_call x1, Pallas kernels: 14.7 us -> 10.6 us  [grads_call(): pl.pallas_call(functools.partial(grads_kernel, head_dim, 8), out_shape=[s...]
where the time goes in v3:
time: 99.9 us; the launch traced here: 99.8 us
  Pallas kernels  99 us (99%)
    pallas_call x1, Pallas kernels, block_call(): pl.pallas_call(functools.partial(block_kernel, n_tp, head_dim, seq_len),...  88.5 us
    pallas_call x1, Pallas kernels, grads_call(): pl.pallas_call(functools.partial(grads_kernel, head_dim, 8), out_shape=[s...  10.6 us

profile of v3, /device:TPU:81, one launch (start us, length us, event | category | flops | bytes accessed | tf_op | source)
XLA Modules:
  0.0 99.8 jit_solution(3791011286324387219)
XLA Ops:
  0.6 88.5 %block_back.1 = (f32[256,2048]{1,0:T(8,128)S(1)}, f32[256,2048]{1,0:T(8,128)S(1)}, f32[256,2048]{1,0:T(8,128)S(1)}, f32[256,2048]{1,0:T(8,128)S(1)}, bf16[256,20...) custom-call(s32[8]{0:T(128)} %lens_ref.1, ...), custom_call_target="tpu_custom_call" | custom-call | flops 10000000000 | bytes 30000000 | tf_op jit(solution)/shard_map/block_back/pallas_call | solution.py:419
  89.1 10.6 %weight_grads.1 = (f32[256,2048]{1,0:T(8,128)}, f32[256,2048]{1,0:T(8,128)}, f32[256,2048]{1,0:T(8,128)}, f32[256,2048]{1,0:T(8,128)}, f32[4096,128]{1,0:T(8,128...) custom-call(f32[256,2048]{1,0:T(8,128)S(1)} %get-tuple-element.31.x2, ...), custom_call_target="tpu_custom_call" | custom-call | flops 4000000000 | bytes 40000000 | tf_op jit(solution)/shard_map/weight_grads/pallas_call | solution.py:485

commit v4 on v3

--- a/solution.py
+++ b/solution.py
@@ -17,20 +17,24 @@
 
 N_CHUNKS = 4
 N_GROUPS = 2
-N_PARTS = 2
 N_SUMS = 4
-N_MSGS = 12
-RECV_SLOT = (0, 1, 2, 3, 3, 3, 3, 4, 5, 6, 6, 7)
-
-LOAD_US = 3.5
-STEP_US = {'G1': 1.0, 'G2': 0.9, 'G3': 0.9, 'G4': 0.6, 'PREP': 1.0, 'ATF': 1.6, 'ATO': 0.6, 'ATB': 2.0, 'ATG': 1.2}
-SUM_US = {'F0': 0.03, 'F1': 0.2, 'F2R': 0.05, 'F2L': 0.05, 'F3': 0.25, 'F4R': 0.03, 'F4L': 0.03, 'F5': 0.03, 'F6': 0.03}
-SENDS = {'F0': (0,), 'F1': (1, 2, 3, 4), 'F2R': (5,), 'F2L': (6,), 'F3': (7, 8), 'F4R': (9,), 'F4L': (10,), 'F5': (11,)}
-RECVS = {'F1': (0,), 'F2R': (1,), 'F2L': (2,), 'F3': (3, 4, 5, 6), 'F4R': (7,), 'F4L': (8,), 'F5': (9, 10), 'F6': (11,)}
-AFTER = {'F1': ('F0',), 'F2R': ('F1',), 'F2L': ('F1',), 'F3': ('F2R', 'F2L'), 'F4R': ('F3',), 'F4L': ('F3',),
-         'F5': ('F4R', 'F4L'), 'F6': ('F5',)}
-MSG_US = ((1.5, 1.0),) + ((2.8, 1.9),) * 6 + ((5.6, 1.9),) * 2 + ((2.8, 1.9),) * 2 + ((1.5, 1.0),)
+N_MSGS = 16
+RECV_SLOT = (0, 1, 2, 3, 3, 3, 3, 4, 5, 6, 6, 7, 8, 7, 7, 7)
+
+LOAD_US = 4.0
+STEP_US = {'G1': 0.8, 'G2': 0.4, 'G3': 0.7, 'G4': 0.6, 'PREP': 1.0, 'ATF': 1.6, 'ATO': 0.3, 'ATB': 2.0, 'ATG': 0.6}
+SUM_US = {'F0A': 0.03, 'F0B': 0.03, 'F1A': 0.1, 'F1B': 0.1, 'F2R': 0.05, 'F2L': 0.05, 'F3': 0.25, 'F4R': 0.03,
+          'F4L': 0.03, 'F5': 0.03, 'F6': 0.03}
+SENDS = {'F0A': (0,), 'F0B': (12,), 'F1A': (1, 4), 'F1B': (2, 3), 'F2R': (5,), 'F2L': (6,), 'F3': (7, 8, 11),
+         'F4R': (9, 13), 'F4L': (10, 14), 'F5': (15,)}
+RECVS = {'F1A': (0,), 'F1B': (12,), 'F2R': (1,), 'F2L': (2,), 'F3': (3, 4, 5, 6), 'F4R': (7,), 'F4L': (8,), 'F5': (9, 10),
+         'F6': (11, 13, 14, 15)}
+AFTER = {'F1A': ('F0A',), 'F1B': ('F0B',), 'F2R': ('F1A',), 'F2L': ('F1B',), 'F3': ('F2R', 'F2L'), 'F4R': ('F3',),
+         'F4L': ('F3',), 'F5': ('F4R', 'F4L'), 'F6': ('F5',)}
+MSG_US = ((0.8, 1.0),) + ((2.8, 1.9),) * 6 + ((5.6, 1.9),) * 2 + ((2.8, 1.9),) * 2 + ((0.4, 1.0), (0.8, 1.0)) + ((0.4, 1.0),) * 3
+SAME_CHIP = (0, 11, 12, 13, 14, 15)
 RANK = ('G1', 'G2', 'ATF', 'ATO', 'ATB', 'ATG', 'G3', 'G4', 'PREP')
+BACKLOG_US = 5
 
 
 def plan_order():
@@ -42,33 +46,39 @@
 
     for g in range(N_GROUPS):
         chunks = range(g * per, (g + 1) * per)
-        add(('G1', g), [])
-        add(('G2', g), [('G1', g)])
+        add(('G1', g), [('G2', g - 1, 1)] if g else [])
         add(('ATF', g), [('F6', 0, c) for c in chunks] + [('PREP',)])
-        add(('ATO', g), [('ATF', g)])
         add(('ATB', g), [('F6', 1, c) for c in chunks] + [('ATF', g)])
-        add(('ATG', g), [('ATB', g)])
-    for j in range(N_PARTS):
+        for j in range(2):
+            add(('G2', g, j), [('G1', g)])
+            add(('ATO', g, j), [('ATF', g)])
+            add(('ATG', g, j), [('ATB', g)])
+    for j in range(2):
         add(('G3', j), [('G1', g) for g in range(N_GROUPS)])
-        add(('G4', j), [('G3', k) for k in range(N_PARTS)])
-    add(('PREP',), [('G4', j) for j in range(N_PARTS)])
+        add(('G4', j), [('G3', 0), ('G3', 1)])
+    add(('PREP',), [('G4', 0), ('G4', 1)])
     for c in range(N_CHUNKS):
         g = c // per
-        source = ([('G2', g)], [('G4', j) for j in range(N_PARTS)], [('ATO', g)], [('ATG', g)])
         for a in range(N_SUMS):
             for name in SUM_US:
                 needs = [(p, a, c) for p in AFTER.get(name, ())] + [(i, a, c) for i in RECVS.get(name, ())]
-                add((name, a, c), needs + source[a] if name == 'F0' else needs, SENDS.get(name, ()))
+                if name in ('F0A', 'F0B'):
+                    j = int(name == 'F0B')
+                    needs.append((('G2', g, j), ('G4', j), ('ATO', g, j), ('ATG', g, j))[a])
+                add((name, a, c), needs, SENDS.get(name, ()))
 
     def rank(key):
         if key[0] in STEP_US:
-            pos = RANK.index(key[0])
-            return (-1, key[1], pos) if pos < 2 else (1, pos) + key[1:]
+            return (1, RANK.index(key[0])) + key[1:]
         return (0,) + key[1:] + (key[0],)
 
     now, order, done, free = LOAD_US, [], {}, {}
     while todo:
-        ready = {k: max([done[n] for n in v[0]], default=0.0) for k, v in todo.items() if all(n in done for n in v[0])}
+        ready = {}
+        for key, (needs, _, sends) in todo.items():
+            if all(n in done for n in needs):
+                queue = max([free.get(1 + i % 2, 0.0) for i in sends if i not in SAME_CHIP], default=0.0)
+                ready[key] = max([done[n] for n in needs] + [queue - BACKLOG_US])
         now = max(now, min(ready.values()))
         key = min((k for k, at in ready.items() if at <= now), key=rank)
         _, cost, sends = todo.pop(key)
@@ -76,7 +86,7 @@
         done[key] = now
         order.append(key)
         for i in sends:
-            link = 0 if i in (0, 11) else 1 + i % 2
+            link = 0 if i in SAME_CHIP else 1 + i % 2
             wire, delay = MSG_US[i]
             start = max(now, free.get(link, 0.0))
             free[link] = start + wire / N_CHUNKS
@@ -157,25 +167,34 @@
 
     n_blk = ff // 256
 
-    def load_all():
+    free_sems = list(range(16))
+
+    def load(name, *copies):
+        sem = load_sem.at[free_sems.pop(0)]
+        for src, dst in copies:
+            pltpu.make_async_copy(src, dst, sem).start()
+        whole = copies[0][1] if len(copies) == 1 else {'y2': y2_own, 'dy1': dy1_own}[name[0]]
+        loads[name] = pltpu.make_async_copy(whole, whole, sem)
+
+    def load_first():
         groups = [pl.ds(g * (tokens // N_GROUPS), tokens // N_GROUPS) for g in range(N_GROUPS)]
-        blocks = [pl.ds(j * 256, 256) for j in range(n_blk)]
-        todo = [(('y1', 0), y1_hbm.at[groups[0]], y1.at[groups[0]])]
-        todo += [(('w1', j), w1_hbm.at[:, blk], w1.at[:, blk]) for j, blk in enumerate(blocks)]
-        todo += [(('y1', g), y1_hbm.at[groups[g]], y1.at[groups[g]]) for g in range(1, N_GROUPS)]
-        todo += [(('w2',), w2_hbm, w2), (('dy2',), dy2_hbm, dy2)]
-        todo += [(('wq',), wq_hbm, wq_raw),
-                 (('wk',), wk_hbm, wqkv.at[:, pl.ds(qdim, head_dim)]),
-                 (('wv',), wv_hbm, wqkv.at[:, pl.ds(qdim + head_dim, head_dim)]),
-                 (('wo',), wo_hbm, wo)]
-        for i, (name, src, dst) in enumerate(todo):
-            loads[name] = pltpu.make_async_copy(src, dst, load_sem.at[i])
-            loads[name].start()
-            if name == ('dy2',):
-                for k, src_hbm, own in ((14, y2_hbm, y2_own), (15, dy1_hbm, dy1_own)):
-                    for c in range(N_CHUNKS):
-                        pltpu.make_async_copy(src_hbm.at[piece_rows(c, chip)], own.at[own_rows(c)], load_sem.at[k]).start()
-                    loads['own', k] = pltpu.make_async_copy(own, own, load_sem.at[k])
+        load(('y1', 0), (y1_hbm.at[groups[0]], y1.at[groups[0]]))
+        for j in range(n_blk):
+            blk = pl.ds(j * 256, 256)
+            load(('w1', j), (w1_hbm.at[:, blk], w1.at[:, blk]))
+        for j, cols in enumerate((lo, hi)):
+            load(('w2', j), (w2_hbm.at[:, cols], w2.at[:, cols]))
+        for g in range(1, N_GROUPS):
+            load(('y1', g), (y1_hbm.at[groups[g]], y1.at[groups[g]]))
+
+    def load_rest():
+        load(('dy2',), (dy2_hbm, dy2))
+        load(('y2',), *((y2_hbm.at[piece_rows(c, chip)], y2_own.at[own_rows(c)]) for c in range(N_CHUNKS)))
+        load(('dy1',), *((dy1_hbm.at[piece_rows(c, chip)], dy1_own.at[own_rows(c)]) for c in range(N_CHUNKS)))
+        load(('wq',), (wq_hbm, wq_raw))
+        load(('wk',), (wk_hbm, wqkv.at[:, pl.ds(qdim, head_dim)]))
+        load(('wv',), (wv_hbm, wqkv.at[:, pl.ds(qdim + head_dim, head_dim)]))
+        load(('wo',), (wo_hbm, wo))
 
     def shared(a, c):
         return a % 2 * N_CHUNKS + c
@@ -186,7 +205,9 @@
         slot = pl.ds(u * piece, piece)
         pa, oa = part.at[a], full[a]
         if i == 0:
-            src, dst, dev = pa.at[half_rows(c, 1 - core)], d2d.at[pl.ds(u * half, half)], partner
+            src, dst, dev = pa.at[half_rows(c, 1 - core), lo], d2d.at[pl.ds(u * half, half), lo], partner
+        elif i == 12:
+            src, dst, dev = pa.at[half_rows(c, 1 - core), hi], d2d.at[pl.ds(u * half, half), hi], partner
         elif i == 1:
             src, dst, dev = pa.at[rows_o, lo], ring1.at[0, slot], right
         elif i == 2:
@@ -208,7 +229,8 @@
         elif i == 10:
             src, dst, dev = oa.at[rows_r, hi], oa.at[rows_r, hi], left
         else:
-            src, dst, dev = oa.at[half_rows(c, core)], oa.at[half_rows(c, core)], partner
+            rows = {11: rows_own, 13: rows_l, 14: rows_r, 15: rows_o}[i]
+            src, dst, dev = oa.at[rows], oa.at[rows], partner
         return pltpu.make_async_remote_copy(src, dst, send_sem.at[i], recv_sem.at[RECV_SLOT[i], shared(a, c)],
                                             device_id={'tp': dev}, device_id_type=MESH)
 
@@ -219,24 +241,40 @@
     def recv(a, c, *slots):
         u = pl.ds((a * N_CHUNKS + c) * piece, piece)
         own = full[a].at[piece_rows(c, chip)]
-        whole = (d2d.at[pl.ds((a * N_CHUNKS + c) * half, half)], ring1.at[0, u], ring1.at[1, u], ring2.at[:, u],
-                 own, own, own, full[a].at[half_rows(c, core)])
+        pair = pl.ds((a * N_CHUNKS + c) * half, half)
+        whole = (d2d.at[pair, lo], ring1.at[0, u], ring1.at[1, u], ring2.at[:, u],
+                 own, own, own, full[a].at[half_rows(c, core)], d2d.at[pair, hi])
         for s in slots:
             pltpu.make_async_copy(whole[s], whole[s], recv_sem.at[s, shared(a, c)]).wait()
 
     state = {'met': False}
 
-    def f0(a, c):
+    def met():
         if not state['met']:
             pl.semaphore_wait(barrier, 3)
             state['met'] = True
+
+    def f0a(a, c):
+        met()
         send(a, c, 0)
 
-    def f1(a, c):
+    def f0b(a, c):
+        met()
+        send(a, c, 12)
+
+    def add_pair(a, c, cols):
+        rows = half_rows(c, core)
+        part[a, rows, cols] = part[a, rows, cols] + d2d[pl.ds((a * N_CHUNKS + c) * half, half), cols]
+
+    def f1a(a, c):
         recv(a, c, 0)
-        rows = half_rows(c, core)
-        part[a, rows] = part[a, rows] + d2d[pl.ds((a * N_CHUNKS + c) * half, half)]
-        send(a, c, 1, 2, 3, 4)
+        add_pair(a, c, lo)
+        send(a, c, 1, 4)
+
+    def f1b(a, c):
+        recv(a, c, 8)
+        add_pair(a, c, hi)
+        send(a, c, 2, 3)
 
     def f2r(a, c):
         recv(a, c, 1)
@@ -256,29 +294,29 @@
         slot = pl.ds((a * N_CHUNKS + c) * piece, piece)
         total = part[a, rows] + ring2[0, slot] + ring2[1, slot]
         if a == 0:
-            arrived(('own', 14))
+            arrived(('y2',))
             out = y2_own[own_rows(c)] - total
         elif a == 1:
-            arrived(('own', 15))
+            arrived(('dy1',))
             out = dy1_own[own_rows(c)] + rms_back(y1[rows], total)
         elif a == 2:
             out = y1[rows] - total
         else:
             out = dy2[rows] + rms_back(x2[rows], total)
         full[a][rows] = out
-        send(a, c, 7, 8)
+        send(a, c, 7, 8, 11)
 
     def f4r(a, c):
         recv(a, c, 4)
-        send(a, c, 9)
+        send(a, c, 9, 13)
 
     def f4l(a, c):
         recv(a, c, 5)
-        send(a, c, 10)
+        send(a, c, 10, 14)
 
     def f5(a, c):
         recv(a, c, 6)
-        send(a, c, 11)
+        send(a, c, 15)
 
     def f6(a, c):
         recv(a, c, 7)
@@ -302,20 +340,22 @@
             dact[rows, cols] = 0.5 * (1.0 + th) + (0.5 * pre) * (1.0 - th * th) * (
                 GELU_C * (1.0 + (3.0 * GELU_A) * (pre * pre)))
 
-    def g2(g):
-        rows = group_rows(g)
-        arrived(('w2',))
-        part[0, rows] = mm(act[rows], w2[...])
+    def g2(g, j):
+        rows, cols = group_rows(g), (lo, hi)[j]
+        arrived(('w2', j))
+        if g == 0 and j == 1:
+            load_rest()
+        part[0, rows, cols] = mm(act[rows], w2[:, cols])
 
     def g3(j):
         arrived(('dy2',))
-        cols = pl.ds(j * (ff // N_PARTS), ff // N_PARTS)
+        cols = pl.ds(j * (ff // 2), ff // 2)
         if j == 0:
             dyb[...] = dy2[...].astype(BF16)
         dpre[:, cols] = (dact[:, cols] * mm_nt(dyb[...], w2[cols])).astype(BF16)
 
     def g4(j):
-        cols = pl.ds(j * (width // N_PARTS), width // N_PARTS)
+        cols = (lo, hi)[j]
         part[1, :, cols] = mm_nt(dpre[...], w1[cols])
 
     def prep():
@@ -350,10 +390,10 @@
             prob[h, rows] = probs
             attn[rows, cols] = mm(probs.astype(BF16), val).astype(BF16)
 
-    def ato(g):
-        rows = group_rows(g)
+    def ato(g, j):
+        rows, cols = group_rows(g), (lo, hi)[j]
         arrived(('wo',))
-        part[2, rows] = mm(attn[rows], wo[...])
+        part[2, rows, cols] = mm(attn[rows], wo[:, cols])
 
     def atb(g):
         rows = group_rows(g)
@@ -375,16 +415,17 @@
         dqkv[rows, pl.ds(qdim, head_dim)] = d_key.astype(BF16)
         dqkv[rows, pl.ds(qdim + head_dim, head_dim)] = d_val.astype(BF16)
 
-    def atg(g):
-        rows = group_rows(g)
-        part[3, rows] = mm_nt(dqkv[rows], wqkv[...])
-
-    steps = {'F0': f0, 'F1': f1, 'F2R': f2r, 'F2L': f2l, 'F3': f3, 'F4R': f4r, 'F4L': f4l, 'F5': f5, 'F6': f6,
+    def atg(g, j):
+        rows, cols = group_rows(g), (lo, hi)[j]
+        part[3, rows, cols] = mm_nt(dqkv[rows], wqkv[cols])
+
+    steps = {'F0A': f0a, 'F0B': f0b, 'F1A': f1a, 'F1B': f1b, 'F2R': f2r, 'F2L': f2l, 'F3': f3, 'F4R': f4r, 'F4L': f4l, 'F5': f5, 'F6': f6,
              'G1': g1, 'G2': g2, 'G3': g3, 'G4': g4, 'PREP': prep, 'ATF': atf, 'ATO': ato, 'ATB': atb, 'ATG': atg}
-    load_all()
+    load_first()
     for name, *where in plan_order():
         steps[name](*where)
-    sent = (d2d,) + (ring1.at[0],) * 6 + (ring2.at[0],) * 2 + (ring1.at[0],) * 2 + (d2d,)
+    sent = ((d2d.at[:, lo],) + (ring1.at[0],) * 6 + (ring2.at[0],) * 2 + (ring1.at[0],) * 2
+            + (ring2.at[0], d2d.at[:, hi]) + (ring2.at[0],) * 3)
     for i in range(N_MSGS):
         pltpu.make_async_copy(sent[i], sent[i], send_sem.at[i]).wait()
 
@@ -414,7 +455,7 @@
         vm((tokens, ff), F32), vm((tokens, qkv_dim), BF16), vm((n_heads, tokens, tokens // N_GROUPS), F32),
         vm((N_SUMS, tokens, width), F32), vm((units * half, width), F32),
         vm((2, units * piece, width // 2), F32), vm((2, units * piece, width), F32),
-        pltpu.SemaphoreType.DMA((16,)), pltpu.SemaphoreType.DMA((N_MSGS,)), pltpu.SemaphoreType.DMA((8, units // 2)),
+        pltpu.SemaphoreType.DMA((16,)), pltpu.SemaphoreType.DMA((N_MSGS,)), pltpu.SemaphoreType.DMA((9, units // 2)),
     ]
     return pl.pallas_call(
         functools.partial(block_kernel, n_tp, head_dim, seq_len),

time: 99.9 us -> 95.7 us (0.958)
  Pallas kernels: 99 us -> 94.8 us
    pallas_call x1, Pallas kernels: 88.5 us -> 84.2 us  [block_call(): pl.pallas_call(functools.partial(block_kernel, n_tp, head_dim, seq_len),...]
where the time goes in v4:
time: 95.7 us; the launch traced here: 95.6 us
  Pallas kernels  94.8 us (99%)
    pallas_call x1, Pallas kernels, block_call(): pl.pallas_call(functools.partial(block_kernel, n_tp, head_dim, seq_len),...  84.2 us
    pallas_call x1, Pallas kernels, grads_call(): pl.pallas_call(functools.partial(grads_kernel, head_dim, 8), out_shape=[s...  10.6 us

profile of v4, /device:TPU:81, one launch (start us, length us, event | category | flops | bytes accessed | tf_op | source)
XLA Modules:
  0.0 95.6 jit_solution(11380241381581662726)
XLA Ops:
  0.6 84.2 %block_back.1 = (f32[256,2048]{1,0:T(8,128)S(1)}, f32[256,2048]{1,0:T(8,128)S(1)}, f32[256,2048]{1,0:T(8,128)S(1)}, f32[256,2048]{1,0:T(8,128)S(1)}, bf16[256,20...) custom-call(s32[8]{0:T(128)} %lens_ref.1, ...), custom_call_target="tpu_custom_call" | custom-call | flops 10000000000 | bytes 30000000 | tf_op jit(solution)/shard_map/block_back/pallas_call | solution.py:460
  84.9 10.6 %weight_grads.1 = (f32[256,2048]{1,0:T(8,128)}, f32[256,2048]{1,0:T(8,128)}, f32[256,2048]{1,0:T(8,128)}, f32[256,2048]{1,0:T(8,128)}, f32[4096,128]{1,0:T(8,128...) custom-call(f32[256,2048]{1,0:T(8,128)S(1)} %get-tuple-element.31.x2, ...), custom_call_target="tpu_custom_call" | custom-call | flops 4000000000 | bytes 40000000 | tf_op jit(solution)/shard_map/weight_grads/pallas_call | solution.py:526

commit v5 on v4

--- a/solution.py
+++ b/solution.py
@@ -22,7 +22,7 @@
 RECV_SLOT = (0, 1, 2, 3, 3, 3, 3, 4, 5, 6, 6, 7, 8, 7, 7, 7)
 
 LOAD_US = 4.0
-STEP_US = {'G1': 0.8, 'G2': 0.4, 'G3': 0.7, 'G4': 0.6, 'PREP': 1.0, 'ATF': 1.6, 'ATO': 0.3, 'ATB': 2.0, 'ATG': 0.6}
+STEP_US = {'G1': 0.7, 'G2': 0.4, 'G3': 0.6, 'G4': 0.5, 'PREP': 0.4, 'ATF': 1.2, 'ATO': 0.2, 'ATB': 1.5, 'ATG': 0.5}
 SUM_US = {'F0A': 0.03, 'F0B': 0.03, 'F1A': 0.1, 'F1B': 0.1, 'F2R': 0.05, 'F2L': 0.05, 'F3': 0.25, 'F4R': 0.03,
           'F4L': 0.03, 'F5': 0.03, 'F6': 0.03}
 SENDS = {'F0A': (0,), 'F0B': (12,), 'F1A': (1, 4), 'F1B': (2, 3), 'F2R': (5,), 'F2L': (6,), 'F3': (7, 8, 11),
@@ -31,10 +31,13 @@
          'F6': (11, 13, 14, 15)}
 AFTER = {'F1A': ('F0A',), 'F1B': ('F0B',), 'F2R': ('F1A',), 'F2L': ('F1B',), 'F3': ('F2R', 'F2L'), 'F4R': ('F3',),
          'F4L': ('F3',), 'F5': ('F4R', 'F4L'), 'F6': ('F5',)}
-MSG_US = ((0.8, 1.0),) + ((2.8, 1.9),) * 6 + ((5.6, 1.9),) * 2 + ((2.8, 1.9),) * 2 + ((0.4, 1.0), (0.8, 1.0)) + ((0.4, 1.0),) * 3
+MSG_US = ((0.8, 1.1),) + ((2.8, 2.17),) * 6 + ((5.6, 2.17),) * 2 + ((2.8, 2.17),) * 2 + ((0.4, 1.1), (0.8, 1.1)) + ((0.4, 1.1),) * 3
 SAME_CHIP = (0, 11, 12, 13, 14, 15)
 RANK = ('G1', 'G2', 'ATF', 'ATO', 'ATB', 'ATG', 'G3', 'G4', 'PREP')
-BACKLOG_US = 5
+BACKLOG_US = (8.7, 4.2, 2.5, 11.5)
+STEP_RANK = {'F0A': 5.4, 'F0B': -2.2, 'F1A': -0.2, 'F1B': -7.9, 'F2R': 5.1, 'F2L': 1.2, 'F3': 2.0, 'F4R': -3.8, 'F4L': -1.6, 'F5': -8.6, 'F6': 1.8}
+SUM_RANK = (2.9, 6.4, 2.0, 13.4)
+CHUNK_RANK = 4.27
 
 
 def plan_order():
@@ -70,7 +73,7 @@
     def rank(key):
         if key[0] in STEP_US:
             return (1, RANK.index(key[0])) + key[1:]
-        return (0,) + key[1:] + (key[0],)
+        return (0, STEP_RANK[key[0]] + SUM_RANK[key[1]] + CHUNK_RANK * key[2])
 
     now, order, done, free = LOAD_US, [], {}, {}
     while todo:
@@ -78,7 +81,7 @@
         for key, (needs, _, sends) in todo.items():
             if all(n in done for n in needs):
                 queue = max([free.get(1 + i % 2, 0.0) for i in sends if i not in SAME_CHIP], default=0.0)
-                ready[key] = max([done[n] for n in needs] + [queue - BACKLOG_US])
+                ready[key] = max([done[n] for n in needs] + [queue - (BACKLOG_US[key[1]] if sends else 0.0)])
         now = max(now, min(ready.values()))
         key = min((k for k, at in ready.items() if at <= now), key=rank)
         _, cost, sends = todo.pop(key)

time: 95.7 us -> 92.7 us (0.969)
  Pallas kernels: 94.8 us -> 91.8 us
    pallas_call x1, Pallas kernels: 84.2 us -> 81.2 us  [block_call(): pl.pallas_call(functools.partial(block_kernel, n_tp, head_dim, seq_len),...]
where the time goes in v5:
time: 92.7 us; the launch traced here: 92.6 us
  Pallas kernels  91.8 us (99%)
    pallas_call x1, Pallas kernels, block_call(): pl.pallas_call(functools.partial(block_kernel, n_tp, head_dim, seq_len),...  81.2 us
    pallas_call x1, Pallas kernels, grads_call(): pl.pallas_call(functools.partial(grads_kernel, head_dim, 8), out_shape=[s...  10.6 us

profile of v5, /device:TPU:81, one launch (start us, length us, event | category | flops | bytes accessed | tf_op | source)
XLA Modules:
  0.0 92.6 jit_solution(9601112378549000467)
XLA Ops:
  0.6 81.2 %block_back.1 = (f32[256,2048]{1,0:T(8,128)S(1)}, f32[256,2048]{1,0:T(8,128)S(1)}, f32[256,2048]{1,0:T(8,128)S(1)}, f32[256,2048]{1,0:T(8,128)S(1)}, bf16[256,20...) custom-call(s32[8]{0:T(128)} %lens_ref.1, ...), custom_call_target="tpu_custom_call" | custom-call | flops 10000000000 | bytes 30000000 | tf_op jit(solution)/shard_map/block_back/pallas_call | solution.py:463
  81.9 10.6 %weight_grads.1 = (f32[256,2048]{1,0:T(8,128)}, f32[256,2048]{1,0:T(8,128)}, f32[256,2048]{1,0:T(8,128)}, f32[256,2048]{1,0:T(8,128)}, f32[4096,128]{1,0:T(8,128...) custom-call(f32[256,2048]{1,0:T(8,128)S(1)} %get-tuple-element.31.x2, ...), custom_call_target="tpu_custom_call" | custom-call | flops 4000000000 | bytes 40000000 | tf_op jit(solution)/shard_map/weight_grads/pallas_call | solution.py:529

commit v6 on v5

--- a/solution.py
+++ b/solution.py
@@ -19,6 +19,7 @@
 N_GROUPS = 2
 N_SUMS = 4
 N_MSGS = 16
+SEND_SLOT = (0, 0, 0, 0, 0, 0, 0, 1, 1, 0, 0, 1, 0, 1, 1, 1)
 RECV_SLOT = (0, 1, 2, 3, 3, 3, 3, 4, 5, 6, 6, 7, 8, 7, 7, 7)
 
 LOAD_US = 4.0
@@ -120,11 +121,11 @@
 
 
 def block_kernel(n_tp, head_dim, seq_len,
-                 lens_ref, y1_hbm, y2_hbm, dy1_hbm, dy2_hbm, wq_hbm, wk_hbm, wv_hbm, wo_hbm, w1_hbm, w2_hbm,
+                 lens_hbm, y1_hbm, y2_hbm, dy1_hbm, dy2_hbm, wq_hbm, wk_hbm, wv_hbm, wo_hbm, w1_hbm, w2_hbm,
                  x2, dx1, x1, dx2, ng, nf, act, dpre, attn, dqkv, dyb,
                  w1, w2, wqkv, wo, wq_raw, wq_f, y1, dy2, y2_own, dy1_own, dact, qkv, prob,
                  part, d2d, ring1, ring2,
-                 load_sem, send_sem, recv_sem):
+                 lens, load_sem, send_sem, recv_sem):
     full = (x2, dx1, x1, dx2)
     tokens, width = y1.shape
     ff = w1.shape[1]
@@ -168,9 +169,9 @@
             if name in loads:
                 loads.pop(name).wait()
 
-    n_blk = ff // 256
-
-    free_sems = list(range(16))
+    n_blk = ff // 512
+
+    free_sems = list(range(14))
 
     def load(name, *copies):
         sem = load_sem.at[free_sems.pop(0)]
@@ -183,7 +184,7 @@
         groups = [pl.ds(g * (tokens // N_GROUPS), tokens // N_GROUPS) for g in range(N_GROUPS)]
         load(('y1', 0), (y1_hbm.at[groups[0]], y1.at[groups[0]]))
         for j in range(n_blk):
-            blk = pl.ds(j * 256, 256)
+            blk = pl.ds(j * 512, 512)
             load(('w1', j), (w1_hbm.at[:, blk], w1.at[:, blk]))
         for j, cols in enumerate((lo, hi)):
             load(('w2', j), (w2_hbm.at[:, cols], w2.at[:, cols]))
@@ -198,6 +199,7 @@
         load(('wk',), (wk_hbm, wqkv.at[:, pl.ds(qdim, head_dim)]))
         load(('wv',), (wv_hbm, wqkv.at[:, pl.ds(qdim + head_dim, head_dim)]))
         load(('wo',), (wo_hbm, wo))
+        load(('lens',), (lens_hbm, lens))
 
     def shared(a, c):
         return a % 2 * N_CHUNKS + c
@@ -234,7 +236,7 @@
         else:
             rows = {11: rows_own, 13: rows_l, 14: rows_r, 15: rows_o}[i]
             src, dst, dev = oa.at[rows], oa.at[rows], partner
-        return pltpu.make_async_remote_copy(src, dst, send_sem.at[i], recv_sem.at[RECV_SLOT[i], shared(a, c)],
+        return pltpu.make_async_remote_copy(src, dst, send_sem.at[SEND_SLOT[i]], recv_sem.at[RECV_SLOT[i], shared(a, c)],
                                             device_id={'tp': dev}, device_id_type=MESH)
 
     def send(a, c, *ids):
@@ -335,7 +337,7 @@
         y_val = y1[rows]
         ng[rows] = (y_val * inv_rms(y_val)).astype(BF16)
         for j in range(n_blk):
-            cols = pl.ds(j * 256, 256)
+            cols = pl.ds(j * 512, 512)
             arrived(('w1', j))
             pre = mm(ng[rows], w1[:, cols])
             th = jnp.tanh(GELU_C * (pre + GELU_A * (pre * pre * pre)))
@@ -369,7 +371,7 @@
 
     def atf(g):
         rows = group_rows(g)
-        arrived(('wk',), ('wv',))
+        arrived(('wk',), ('wv',), ('lens',))
         x_val = x2[rows]
         nf[rows] = (x_val * inv_rms(x_val)).astype(BF16)
         qkv[rows] = mm(nf[rows], wqkv[...]).astype(BF16)
@@ -381,7 +383,7 @@
         visible = jnp.zeros((group, group), jnp.bool_)
         for s in range(n_seqs):
             base = s * seq_len
-            stop = base + lens_ref[g * n_seqs + s]
+            stop = base + lens[g * n_seqs + s]
             visible = visible | ((row_pos >= base) & (row_pos < base + seq_len)
                                  & (col_pos >= base) & (col_pos < stop) & (col_pos <= row_pos))
         for h in range(n_heads):
@@ -427,10 +429,8 @@
     load_first()
     for name, *where in plan_order():
         steps[name](*where)
-    sent = ((d2d.at[:, lo],) + (ring1.at[0],) * 6 + (ring2.at[0],) * 2 + (ring1.at[0],) * 2
-            + (ring2.at[0], d2d.at[:, hi]) + (ring2.at[0],) * 3)
-    for i in range(N_MSGS):
-        pltpu.make_async_copy(sent[i], sent[i], send_sem.at[i]).wait()
+    for i, sent in enumerate((part, part.at[pl.ds(0, 3)])):
+        pltpu.make_async_copy(sent, sent, send_sem.at[i]).wait()
 
 
 def block_call(n_tp, seq_lens, y_one, y_two, dy_one, dy_two, w_query, w_key, w_value, w_out, w_up, w_down):
@@ -458,12 +458,12 @@
         vm((tokens, ff), F32), vm((tokens, qkv_dim), BF16), vm((n_heads, tokens, tokens // N_GROUPS), F32),
         vm((N_SUMS, tokens, width), F32), vm((units * half, width), F32),
         vm((2, units * piece, width // 2), F32), vm((2, units * piece, width), F32),
-        pltpu.SemaphoreType.DMA((16,)), pltpu.SemaphoreType.DMA((N_MSGS,)), pltpu.SemaphoreType.DMA((9, units // 2)),
+        pltpu.SMEM((n_batch,), jnp.int32), pltpu.SemaphoreType.DMA((14,)), pltpu.SemaphoreType.DMA((2,)), pltpu.SemaphoreType.DMA((9, units // 2)),
     ]
     return pl.pallas_call(
         functools.partial(block_kernel, n_tp, head_dim, seq_len),
         out_shape=out_shape,
-        in_specs=[pl.BlockSpec(memory_space=pltpu.SMEM)] + [ANY] * 10,
+        in_specs=[ANY] * 11,
         out_specs=[pl.BlockSpec(memory_space=pltpu.VMEM)] * len(out_shape),
         scratch_shapes=scratch,
         name='block_back',
@@ -477,14 +477,15 @@
                  x2, dx1, x1, dx2, ng, nf, act, dpre, attn, dqkv, e_val,
                  x2_out, dx1_out, x1_out, dx2_out, dwq_out, dwk_out, dwv_out, dwo_out, dw1_out, dw2_out,
                  c_val, dwq, dwk, dwv, dwo, dw1, dw2, out_sem):
-    outs = []
-
-    def store(src, dst):
-        outs.append(pltpu.make_async_copy(src, dst, out_sem.at[len(outs)]))
-        outs[-1].start()
-
-    store(x2, x2_out)
-    store(dx1, dx1_out)
+    pairs = ((x2, x2_out), (dx1, dx1_out), (x1, x1_out), (dx2, dx2_out), (dw2, dw2_out), (dw1, dw1_out),
+             (dwo, dwo_out), (dwq, dwq_out), (dwk, dwk_out), (dwv, dwv_out))
+
+    def store(i, rows=None):
+        src, dst = pairs[i] if rows is None else (ref.at[rows] for ref in pairs[i])
+        pltpu.make_async_copy(src, dst, out_sem.at[i]).start()
+
+    store(0)
+    store(1)
     width, ff = dw1.shape
     qdim = attn.shape[1]
     n_heads = qdim // head_dim
@@ -492,18 +493,18 @@
     for j in range(n_blk):
         rows = pl.ds(j * rows2, rows2)
         dw2[rows] = mm_tn(act[:, rows], e_val[...])
-        store(dw2.at[rows], dw2_out.at[rows])
+        store(4, rows)
     for j in range(n_blk):
         rows = pl.ds(j * rows1, rows1)
         dw1[rows] = mm_tn(ng[:, rows], dpre[...])
-        store(dw1.at[rows], dw1_out.at[rows])
-    store(x1, x1_out)
-    store(dx2, dx2_out)
+        store(5, rows)
+    store(2)
+    store(3)
     c_val[...] = dx1[...].astype(BF16)
     for h in range(n_heads):
         rows = pl.ds(h * head_dim, head_dim)
         dwo[rows] = mm_tn(attn[:, rows], c_val[...])
-        store(dwo.at[rows], dwo_out.at[rows])
+        store(6, rows)
     for j in range(n_blk // 2):
         step = width // (n_blk // 2)
         rows = pl.ds(j * step, step)
@@ -513,11 +514,11 @@
         dwk[rows] = grad[:, qdim:qdim + head_dim]
         dwv[rows] = grad[:, qdim + head_dim:]
         rows_q = pl.ds(j * step * n_heads, step * n_heads)
-        store(dwq.at[rows_q], dwq_out.at[rows_q])
-        store(dwk.at[rows], dwk_out.at[rows])
-        store(dwv.at[rows], dwv_out.at[rows])
-    for copy in outs:
-        copy.wait()
+        store(7, rows_q)
+        store(8, rows)
+        store(9, rows)
+    for i, (src, dst) in enumerate(pairs):
+        pltpu.make_async_copy(src, dst, out_sem.at[i]).wait()
 
 
 def grads_call(n_heads, head_dim, *saved):
@@ -525,7 +526,7 @@
     ff, qdim = saved[6].shape[1], n_heads * head_dim
     sds, vm = jax.ShapeDtypeStruct, pltpu.VMEM
     dw_shapes = [(width * n_heads, head_dim), (width, head_dim), (width, head_dim), (qdim, width), (width, ff), (ff, width)]
-    scratch = [vm((tokens, width), BF16)] + [vm(s, F32) for s in dw_shapes] + [pltpu.SemaphoreType.DMA((40,))]
+    scratch = [vm((tokens, width), BF16)] + [vm(s, F32) for s in dw_shapes] + [pltpu.SemaphoreType.DMA((10,))]
     return pl.pallas_call(
         functools.partial(grads_kernel, head_dim, 8),
         out_shape=[sds((tokens, width), F32)] * 4 + [sds(s, F32) for s in dw_shapes],

time: 92.7 us -> 91.5 us (0.987)
  Pallas kernels: 91.8 us -> 90.6 us
    pallas_call x1, Pallas kernels: 81.2 us -> 80.3 us  [block_call(): pl.pallas_call(functools.partial(block_kernel, n_tp, head_dim, seq_len),...]
where the time goes in v6:
time: 91.5 us; the launch traced here: 91.4 us
  Pallas kernels  90.6 us (99%)
    pallas_call x1, Pallas kernels, block_call(): pl.pallas_call(functools.partial(block_kernel, n_tp, head_dim, seq_len),...  80.3 us
    pallas_call x1, Pallas kernels, grads_call(): pl.pallas_call(functools.partial(grads_kernel, head_dim, 8), out_shape=[s...  10.3 us

profile of v6, /device:TPU:81, one launch (start us, length us, event | category | flops | bytes accessed | tf_op | source)
XLA Modules:
  0.0 91.4 jit_solution(10418349076820759797)
XLA Ops:
  0.6 80.3 %block_back.1 = (f32[256,2048]{1,0:T(8,128)S(1)}, f32[256,2048]{1,0:T(8,128)S(1)}, f32[256,2048]{1,0:T(8,128)S(1)}, f32[256,2048]{1,0:T(8,128)S(1)}, bf16[256,20...) custom-call(s32[8]{0:T(128)} %lens_hbm.1, ...), custom_call_target="tpu_custom_call" | custom-call | flops 10000000000 | bytes 30000000 | tf_op jit(solution)/shard_map/block_back/pallas_call | solution.py:463
  80.9 10.3 %weight_grads.1 = (f32[256,2048]{1,0:T(8,128)}, f32[256,2048]{1,0:T(8,128)}, f32[256,2048]{1,0:T(8,128)}, f32[256,2048]{1,0:T(8,128)}, f32[4096,128]{1,0:T(8,128...) custom-call(f32[256,2048]{1,0:T(8,128)S(1)} %get-tuple-element.31.x2, ...), custom_call_target="tpu_custom_call" | custom-call | flops 4000000000 | bytes 40000000 | tf_op jit(solution)/shard_map/weight_grads/pallas_call | solution.py:530

commit v7 on v6

--- a/solution.py
+++ b/solution.py
@@ -157,10 +157,6 @@
         return pl.ds(c * piece, piece)
 
     lo, hi = pl.ds(0, hw), pl.ds(hw, hw)
-
-    barrier = pltpu.get_barrier_semaphore()
-    for dev in (partner, left, right):
-        pl.semaphore_signal(barrier, inc=1, device_id={'tp': dev}, device_id_type=MESH)
 
     loads = {}
 
@@ -427,6 +423,9 @@
     steps = {'F0A': f0a, 'F0B': f0b, 'F1A': f1a, 'F1B': f1b, 'F2R': f2r, 'F2L': f2l, 'F3': f3, 'F4R': f4r, 'F4L': f4l, 'F5': f5, 'F6': f6,
              'G1': g1, 'G2': g2, 'G3': g3, 'G4': g4, 'PREP': prep, 'ATF': atf, 'ATO': ato, 'ATB': atb, 'ATG': atg}
     load_first()
+    barrier = pltpu.get_barrier_semaphore()
+    for dev in (partner, left, right):
+        pl.semaphore_signal(barrier, inc=1, device_id={'tp': dev}, device_id_type=MESH)
     for name, *where in plan_order():
         steps[name](*where)
     for i, sent in enumerate((part, part.at[pl.ds(0, 3)])):

time: 91.5 us -> 91.4 us (level)
  no operation moved by 1% of the time
where the time goes in v7:
time: 91.4 us; the launch traced here: 91.3 us
  Pallas kernels  90.5 us (99%)
    pallas_call x1, Pallas kernels, block_call(): pl.pallas_call(functools.partial(block_kernel, n_tp, head_dim, seq_len),...  80.2 us
    pallas_call x1, Pallas kernels, grads_call(): pl.pallas_call(functools.partial(grads_kernel, head_dim, 8), out_shape=[s...  10.3 us

profile of v7, /device:TPU:81, one launch (start us, length us, event | category | flops | bytes accessed | tf_op | source)
XLA Modules:
  0.0 91.3 jit_solution(17031761443932634498)
XLA Ops:
  0.6 80.2 %block_back.1 = (f32[256,2048]{1,0:T(8,128)S(1)}, f32[256,2048]{1,0:T(8,128)S(1)}, f32[256,2048]{1,0:T(8,128)S(1)}, f32[256,2048]{1,0:T(8,128)S(1)}, bf16[256,20...) custom-call(s32[8]{0:T(128)} %lens_hbm.1, ...), custom_call_target="tpu_custom_call" | custom-call | flops 10000000000 | bytes 30000000 | tf_op jit(solution)/shard_map/block_back/pallas_call | solution.py:462
  80.9 10.3 %weight_grads.1 = (f32[256,2048]{1,0:T(8,128)}, f32[256,2048]{1,0:T(8,128)}, f32[256,2048]{1,0:T(8,128)}, f32[256,2048]{1,0:T(8,128)}, f32[4096,128]{1,0:T(8,128...) custom-call(f32[256,2048]{1,0:T(8,128)S(1)} %get-tuple-element.31.x2, ...), custom_call_target="tpu_custom_call" | custom-call | flops 4000000000 | bytes 40000000 | tf_op jit(solution)/shard_map/weight_grads/pallas_call | solution.py:529
